TPU v7x, 32 devices: a whole 2x2x4 slice. The times are simulated.
32 devices in a mesh: lat: 4 (over y, x), lon: 8 (over z, core).
Axes of the slice: x: 2, y: 2, z: 4, core: 2. Of those that a mesh axis runs over, the one named last changes fastest.
Arguments:
- state: float32 [64, 384, 1104], P('lat', 'lon'), may hold values from -6 to 6
- background: float32 [64, 384, 1104], P('lat', 'lon'), may hold values from -6 to 6
- inv_background: float32 [1104], replicated, may hold values from 0.1 to 1
- w_embed: bfloat16 [1104, 256], replicated, may hold values from -0.1875 to 0.1875
- norm_gain: float32 [2, 2, 256], replicated, may hold values from 0.25 to 1.75
- w_qkv: bfloat16 [2, 256, 768], replicated, may hold values from -0.375 to 0.375
- w_proj: bfloat16 [2, 256, 256], replicated, may hold values from -0.375 to 0.375
- head_scale: float32 [2, 8], replicated, may hold values from 2 to 12
- w_up: bfloat16 [2, 256, 1024], replicated, may hold values from -0.375 to 0.375
- w_down: bfloat16 [2, 1024, 256], replicated, may hold values from -0.1875 to 0.1875
- w_head: bfloat16 [256, 1104], replicated, may hold values from -0.375 to 0.375
- w_obs1: float32 [69, 256], replicated, may hold values from -0.75 to 0.75
- w_obs2: float32 [256, 256], replicated, may hold values from -0.375 to 0.375
- r_inverse: float32 [256, 256], replicated, as said below
- obs_values: float32 [65536, 256], P(('lat', 'lon')), may hold values from -6 to 6
- obs_owner: int32 [65536, 1], P(('lat', 'lon')), may hold values from 0 to 31; in each aligned block of 2048 rows (0 to 2047, 2048 to 4095, ...) at most 128 rows name the same one
- obs_point: int32 [65536], P(('lat', 'lon')), may hold values from 0 to 12287
- obs_count: int32 [32], P(('lat', 'lon')), may hold values from 1024 to 2048, as said below
Outputs:
- gradient: float32 [64, 384, 1104], P('lat', 'lon')
Inputs may be any that keep to these rules, and one draw needn't show every extreme that they name: `r_inverse`: Symmetric, with a positive diagonal larger than the sum of magnitudes of the rest of its row. `obs_owner`: among the slots of one device, at most 128 name the same owner, and in some device exactly 128 do. `obs_count`: some device has all its slots live.
All inputs are finite; a program needn't handle non-finite values.
Results may differ from a plain program's by a relative error of at most 0.018.
Values may be sent and summed in bfloat16 or wider, within the bound.
No kernel may reach another device: no remote copies, remote signals or barrier semaphores. Data moves between devices by JAX's collectives and lax.ppermute only.
A program may use at most 192 MiB of HBM per device.

v0:
```python
import functools

import jax
import jax.numpy as jnp
from jax import lax
from jax.experimental import pallas as pl
from jax.experimental.pallas import tpu as pltpu
from jax.sharding import PartitionSpec as P


HEADS = 8
VARS = 69
PIX = 16
WIN = 8
SHIFT = 4
LANES = 128
EXTRA = 8
EPS = 1e-05
BF = jnp.bfloat16
F32 = jnp.float32
SQRT_2_OVER_PI = 0.7978845608028654
CUBIC = 0.044715

SMEM = pl.BlockSpec(memory_space=pltpu.SMEM)
VMEM = pl.BlockSpec(memory_space=pltpu.VMEM)
HBM = pl.BlockSpec(memory_space=pltpu.HBM)
MIB = 1024 * 1024
ROOM = 44


class Stage:
    def __init__(self):
        self.inputs = {}
        self.outputs = {}
        self.waited = set()
        self.sent = set()

    def need(self, *refs):
        for ref in refs:
            if id(ref) not in self.waited:
                self.waited.add(id(ref))
                self.inputs[id(ref)].wait()

    def need_at(self, first, *refs):
        pending = [ref for ref in refs if id(ref) not in self.waited]
        self.waited.update(id(ref) for ref in pending)

        @pl.when(first)
        def _():
            for ref in pending:
                self.inputs[id(ref)].wait()

    def emit_part(self, part, *refs):
        for ref in refs:
            self.sent.add(id(ref))
            self.outputs[id(ref)].part(part).start()

    def emit(self, *refs):
        for ref in refs:
            if id(ref) not in self.sent:
                self.sent.add(id(ref))
                self.outputs[id(ref)].start()

    def close(self):
        for key, copy in self.inputs.items():
            if key not in self.waited:
                copy.wait()
        for key, copy in self.outputs.items():
            if key not in self.sent:
                copy.start()
        for copy in self.outputs.values():
            copy.wait()


class Outgoing:
    def __init__(self, source, target, sem):
        self.refs = (source, target, sem)

    def part(self, part):
        source, target, sem = self.refs
        return pltpu.make_async_copy(source.at[part], target.at[part], sem)

    def start(self):
        pltpu.make_async_copy(*self.refs).start()

    def wait(self):
        pltpu.make_async_copy(*self.refs).wait()


def staged(
    body, args, outs, scratch, flops, smem=(), raw=(), raw_outs=(), layer=None, vmem=(),
    early=lambda ins, extra: None,
    scalars=(),
):
    layer = layer or {}
    count = len(args)
    placed = [
        x if i in smem or i in vmem else pltpu.with_memory_space_constraint(x, pltpu.HBM)
        for i, x in enumerate(args)
    ]
    in_buffers = []
    for i, x in enumerate(args):
        if i not in smem and i not in raw and i not in vmem:
            shape = x.shape[1:] if i in layer else x.shape
            space = pltpu.SMEM if i in scalars else pltpu.VMEM
            in_buffers.append((i, space(shape, x.dtype)))
    out_buffers = [
        (j, pltpu.VMEM(o.shape, o.dtype)) for j, o in enumerate(outs) if j not in raw_outs
    ]

    def kernel(*refs):
        ins = [
            ref.at[layer[i]] if i in vmem and i in layer else ref
            for i, ref in enumerate(refs[:count])
        ]
        results = list(refs[count : count + len(outs)])
        rest = list(refs[count + len(outs) :])
        ins_vmem = rest[: len(in_buffers)]
        outs_vmem = rest[len(in_buffers) : len(in_buffers) + len(out_buffers)]
        in_sems, out_sems = rest[-2:]
        extra = rest[len(in_buffers) + len(out_buffers) : -2]
        stage = Stage()
        early(ins, extra)
        stage.waited.update(id(ins[i]) for i in vmem)
        for n, ((i, _), buffer) in enumerate(zip(in_buffers, ins_vmem)):
            source = ins[i].at[layer[i]] if i in layer else ins[i]
            copy = pltpu.make_async_copy(source, buffer, in_sems.at[n])
            copy.start()
            stage.inputs[id(buffer)] = copy
            ins[i] = buffer
        for n, ((j, _), buffer) in enumerate(zip(out_buffers, outs_vmem)):
            stage.outputs[id(buffer)] = Outgoing(buffer, results[j], out_sems.at[n])
            results[j] = buffer
        body(stage, *ins, *results, *extra)
        stage.close()

    return pl.pallas_call(
        kernel,
        out_shape=tuple(pltpu.HBM(o.shape, o.dtype) for o in outs),
        in_specs=[
            SMEM if i in smem else VMEM if i in vmem else HBM for i in range(count)
        ],
        out_specs=(HBM,) * len(outs),
        scratch_shapes=[b for _, b in in_buffers]
        + [b for _, b in out_buffers]
        + list(scratch)
        + [
            pltpu.SemaphoreType.DMA((max(1, len(in_buffers)),)),
            pltpu.SemaphoreType.DMA((max(1, len(out_buffers)),)),
        ],
        compiler_params=pltpu.CompilerParams(vmem_limit_bytes=ROOM * MIB),
        cost_estimate=pl.CostEstimate(
            flops=int(flops), bytes_accessed=8 * MIB, transcendentals=0
        ),
    )(*placed)


def scale_lanes(scale_ref, block, width):
    head = lax.broadcasted_iota(jnp.int32, (1, width), 1) // (width // HEADS)
    row = jnp.zeros((1, width), F32)
    for h in range(HEADS):
        row = jnp.where(head == h, scale_ref[block, h], row)
    return row


def nn(a, b):
    return lax.dot_general(a, b, (((1,), (0,)), ((), ())), preferred_element_type=F32)


def nt(a, b):
    return lax.dot_general(a, b, (((1,), (1,)), ((), ())), preferred_element_type=F32)


def tn(a, b):
    return lax.dot_general(a, b, (((0,), (0,)), ((), ())), preferred_element_type=F32)


def norm_parts(h):
    mean = jnp.mean(h, -1, keepdims=True)
    centred = h - mean
    spread = jnp.mean(centred * centred, -1, keepdims=True)
    rstd = lax.rsqrt(spread + EPS)
    return centred * rstd, rstd


def norm(h, gain):
    return (norm_parts(h)[0] * gain).astype(BF)


def norm_back(h, gain, cotangent):
    xhat, rstd = norm_parts(h)
    scaled = cotangent * gain
    m1 = jnp.mean(scaled, -1, keepdims=True)
    m2 = jnp.mean(scaled * xhat, -1, keepdims=True)
    return rstd * (scaled - m1 - xhat * m2)


def gelu_parts(u):
    square = u * u
    t = jnp.tanh(u * (SQRT_2_OVER_PI + SQRT_2_OVER_PI * CUBIC * square))
    half = 0.5 + 0.5 * t
    value = u * half
    rate = 2.0 * SQRT_2_OVER_PI + 6.0 * SQRT_2_OVER_PI * CUBIC * square
    return value, half + value * (1.0 - half) * rate


def head_ones(width, size):
    a = lax.broadcasted_iota(jnp.int32, (width, width), 0) // size
    b = lax.broadcasted_iota(jnp.int32, (width, width), 1) // size
    return (a == b).astype(F32).astype(BF)


def head_stack(tokens, size):
    heads = LANES // size
    a = lax.broadcasted_iota(jnp.int32, (heads * tokens, LANES), 0) // tokens
    b = lax.broadcasted_iota(jnp.int32, (heads * tokens, LANES), 1) // size
    return (a == b).astype(F32).astype(BF)


def stacked(x, mask):
    copies = mask.shape[0] // x.shape[0]
    return [
        jnp.concatenate([x[:, t : t + LANES]] * copies, axis=0) * mask
        for t in range(0, x.shape[1], LANES)
    ]


def scores_of(x, blocks):
    return jnp.concatenate(
        [nt(x[:, t * LANES : (t + 1) * LANES], b) for t, b in enumerate(blocks)], axis=1
    )


def mix_of(p, blocks):
    rows = blocks[0].shape[0]
    return jnp.concatenate(
        [nn(p[:, t * rows : (t + 1) * rows], b) for t, b in enumerate(blocks)], axis=1
    )


def side_mask(window_row, threshold, tokens):
    shape = (tokens, HEADS * tokens)
    a = lax.broadcasted_iota(jnp.int32, shape, 0) // WIN
    b = (lax.broadcasted_iota(jnp.int32, shape, 1) % tokens) // WIN
    first = (window_row * WIN + a) >= threshold
    second = (window_row * WIN + b) >= threshold
    return jnp.where(first == second, 1.0, 0.0).astype(F32)


def window(ref, i, w):
    block = ref[i, :, w, :, :]
    return block.reshape(block.shape[0] * block.shape[1], block.shape[2])


def attention_chunk(qkv, scale, ones_ref, mask_ref, allowed, e_ref, o_ref, count, tokens):
    width = qkv.shape[1] // 3
    q = qkv[:, :width].astype(F32)
    k = qkv[:, width : 2 * width].astype(F32)
    v = qkv[:, 2 * width :]
    ones = ones_ref[...]
    qs = (q * lax.rsqrt(nn((q * q).astype(BF), ones) + 1.0) * scale).astype(BF)
    kn = (k * lax.rsqrt(nn((k * k).astype(BF), ones) + 1.0)).astype(BF)
    mask = mask_ref[...]
    for w in range(count):
        part = slice(w * tokens, (w + 1) * tokens)
        expo = jnp.exp(scores_of(qs[part], stacked(kn[part], mask)))
        if allowed is not None:
            expo = expo * allowed
        expo = expo.astype(BF)
        e_ref[part] = expo
        o_ref[part] = mix_of(expo, stacked(v[part], mask))
    total = mix_of(e_ref[...], [mask] * (width // LANES))
    return (o_ref[...] / total).astype(BF)


def attention_chunk_back(
    qkv, d_out, scale, ones_ref, mask_ref, allowed, dq_ref, dk_ref, dv_ref, count, tokens
):
    width = qkv.shape[1] // 3
    size = width // HEADS
    q = qkv[:, :width].astype(F32)
    k = qkv[:, width : 2 * width].astype(F32)
    v = qkv[:, 2 * width :]
    ones = ones_ref[...]
    rq = lax.rsqrt(nn((q * q).astype(BF), ones) + 1.0)
    rk = lax.rsqrt(nn((k * k).astype(BF), ones) + 1.0)
    qs = (q * rq * scale).astype(BF)
    kn = (k * rk).astype(BF)
    mask = mask_ref[...]
    lane_head = lax.broadcasted_iota(jnp.int32, (1, LANES), 1) // size
    per_tile = LANES // size
    for w in range(count):
        part = slice(w * tokens, (w + 1) * tokens)
        kw = kn[part]
        qm = stacked(qs[part], mask)
        dm = stacked(d_out[part], mask)
        expo = jnp.exp(scores_of(kw, qm))
        if allowed is not None:
            expo = expo * allowed
        p = expo * (1.0 / jnp.sum(expo, 0, keepdims=True))
        dp = scores_of(v[part], dm)
        ds = (p * (dp - jnp.sum(p * dp, 0, keepdims=True))).astype(BF)
        dv_ref[part] = mix_of(p.astype(BF), dm)
        dk_ref[part] = mix_of(ds, qm)
        tiles = []
        for tile in range(width // LANES):
            span = per_tile * tokens
            full = tn(
                ds[:, tile * span : (tile + 1) * span], kw[:, tile * LANES : (tile + 1) * LANES]
            )
            total = None
            for s in range(per_tile):
                block = full[s * tokens : (s + 1) * tokens]
                block = jnp.where(lane_head == s, block, 0.0)
                total = block if total is None else total + block
            tiles.append(total)
        dq_ref[part] = jnp.concatenate(tiles, axis=1)
    dqs = dq_ref[...]
    dkn = dk_ref[...]
    dq = scale * rq * (dqs - q * (rq * rq) * nn((q * dqs).astype(BF), ones))
    dk = rk * (dkn - k * (rk * rk) * nn((k * dkn).astype(BF), ones))
    return jnp.concatenate([dq.astype(BF), dk.astype(BF), dv_ref[...].astype(BF)], axis=1)


def split(cap):
    first = max(8, cap // 4)
    return (first, first, cap - 2 * first), min(16, first)


def route_kernel(
    parts, stage, count_ref, owner_ref, point_ref, r_ref, w2_ref, values_ref,
    send1_ref, send2_ref, send3_ref, mixed_ref, y_ref, buf_ref, tgt_ref, tgt_smem, sem,
):
    cap = sum(parts)
    slots = owner_ref.shape[1]
    devices = send1_ref.shape[0]
    stage.need(owner_ref, point_ref)
    owner = owner_ref[...]
    live = lax.broadcasted_iota(jnp.int32, (1, slots), 1) < count_ref[0]
    match = lax.broadcasted_iota(jnp.int32, (devices, slots), 0) == owner
    match = jnp.where(match, 1.0, 0.0).astype(F32)
    a = lax.broadcasted_iota(jnp.int32, (LANES, LANES), 0)
    b = lax.broadcasted_iota(jnp.int32, (LANES, LANES), 1)
    upper = jnp.where(a < b, 1.0, 0.0).astype(BF)
    chunks = slots // LANES
    flat = jnp.concatenate(
        [match[:, c * LANES : (c + 1) * LANES] for c in range(chunks)], axis=0
    )
    before = nn(flat.astype(BF), upper)
    carry = jnp.zeros((devices, 1), F32)
    ranks = []
    dump = devices * cap
    for c in range(chunks):
        here = match[:, c * LANES : (c + 1) * LANES]
        seen = before[c * devices : (c + 1) * devices] + carry
        ranks.append(jnp.sum(here * seen, 0, keepdims=True))
        span = slice(c * LANES, (c + 1) * LANES)
        spot = owner[:, span] * cap + ranks[-1].astype(jnp.int32)
        tgt_ref[c : c + 1, :] = jnp.where(live[:, span], spot, dump)
        carry = carry + jnp.sum(here, 1, keepdims=True)
    rank = jnp.concatenate(ranks, axis=1).astype(jnp.int32)
    copy = pltpu.make_async_copy(tgt_ref, tgt_smem, sem)
    copy.start()
    place = lax.broadcasted_iota(jnp.int32, (cap, slots), 0) == rank
    place = jnp.where(place & live, 1.0, 0.0).astype(BF)
    point = point_ref[...]
    high = (match * (point // LANES + 1).astype(F32)).astype(BF)
    low = (match * (point % LANES).astype(F32)).astype(BF)
    high = nt(high, place)
    low = nt(low, place)
    stage.need(r_ref, w2_ref, values_ref)
    best = lax.Precision.HIGHEST
    dims = (((1,), (1,)), ((), ()))
    m2 = lax.dot_general(
        r_ref[...], w2_ref[...], dims, precision=best, preferred_element_type=F32
    )
    mixed_ref[...] = jnp.dot(
        w2_ref[...], m2, precision=best, preferred_element_type=F32
    ).astype(BF)
    y = nn(values_ref[...].astype(BF), m2.astype(BF))
    y_ref[0, :, :] = y[:, :LANES]
    y_ref[1, :, :] = y[:, LANES:]
    buf_ref[...] = jnp.zeros_like(buf_ref)
    copy.wait()
    unroll = 16

    def move(c, _):
        base = pl.multiple_of(c * LANES, LANES)
        for start in range(0, LANES, unroll):
            spots = [tgt_smem[c, start + u] for u in range(unroll)]
            for half in range(2):
                for u in range(unroll):
                    buf_ref[half, pl.ds(spots[u], 1), :] = y_ref[
                        half, pl.ds(base + start + u, 1), :
                    ]
        return 0

    lax.fori_loop(0, chunks, move, 0)
    for d in range(devices):
        offset = d * cap
        for ref, size in zip((send1_ref, send2_ref, send3_ref), parts):
            for half in range(2):
                ref[d, 0:size, half * LANES : (half + 1) * LANES] = buf_ref[
                    half, offset : offset + size, :
                ].astype(BF)
            offset += size
    fill = ((0, 0), (0, LANES - cap))
    codes = jnp.concatenate([jnp.pad(high, fill), jnp.pad(low, fill)], axis=1)
    for d in range(devices):
        send1_ref[d, parts[0] : parts[0] + EXTRA, :] = jnp.broadcast_to(
            codes[d : d + 1], (EXTRA, 2 * LANES)
        ).astype(BF)


def route(owner, point, count, values, r_inverse, w2, devices, parts):
    slots, channels = values.shape
    cap = sum(parts)
    sizes = (parts[0] + EXTRA,) + tuple(parts[1:])
    return staged(
        functools.partial(route_kernel, parts),
        (count, owner, point, r_inverse, w2, values),
        tuple(jax.ShapeDtypeStruct((devices, n, channels), BF) for n in sizes)
        + (jax.ShapeDtypeStruct(w2.shape, BF),),
        [
            pltpu.VMEM((2, slots, LANES), F32),
            pltpu.VMEM((2, devices * cap + EXTRA, LANES), F32),
            pltpu.VMEM((slots // LANES, LANES), jnp.int32),
            pltpu.SMEM((slots // LANES, LANES), jnp.int32),
            pltpu.SemaphoreType.DMA,
        ],
        1e9,
        smem=(0,),
    )


def load_state(ins, extra):
    source, target, sems = ins[2], extra[0], extra[-1]
    for i in range(source.shape[0]):
        pltpu.make_async_copy(source.at[i], target.at[i], sems.at[i]).start()


def first_kernel(
    stage, scale_ref, order_ref, state_hbm, we_ref, gain_ref, wqkv_ref, wproj_ref, wup_ref, wdown_ref,
    top_ref, left_ref, corner_ref, z1_ref, h1_ref, h0_ref, hm_ref, qkv_ref, gp_ref,
    state_ref, ones_ref, mask_ref, e_ref, o_ref, sems,
):
    rows, _, cols, _, _ = state_ref.shape
    width = we_ref.shape[1]
    tokens = WIN * WIN
    chunk = cols * tokens

    def load(i):
        return pltpu.make_async_copy(state_hbm.at[i], state_ref.at[i], sems.at[i])

    ones_ref[...] = head_ones(width, width // HEADS)
    mask_ref[...] = head_stack(tokens, width // HEADS)
    scale = scale_lanes(scale_ref, 0, width)
    stage.need(we_ref, gain_ref)

    def body(i, _):
        load(i).wait()
        x = jnp.concatenate([window(state_ref, i, w).astype(BF) for w in range(cols)], axis=0)
        h0 = nn(x, we_ref[...])
        here = pl.ds(pl.multiple_of(i * chunk, chunk), chunk)
        h0_ref[here, :] = h0
        stage.emit_part(here, h0_ref)
        stage.need_at(i == 0, wqkv_ref)
        qkv = nn(norm(h0, gain_ref[0, 0:1]), wqkv_ref[...]).astype(BF)
        qkv_ref[here, :] = qkv
        stage.emit_part(here, qkv_ref)
        mixed = attention_chunk(qkv, scale, ones_ref, mask_ref, None, e_ref, o_ref, cols, tokens)
        stage.need_at(i == 0, wproj_ref, wup_ref, wdown_ref)
        hm = h0 + nn(mixed, wproj_ref[...]).astype(BF).astype(F32)
        hm_ref[here, :] = hm
        stage.emit_part(here, hm_ref)
        inner, slope = gelu_parts(nn(norm(hm, gain_ref[0, 1:2]), wup_ref[...]))
        gp_ref[here, :] = slope.astype(BF)
        stage.emit_part(here, gp_ref)
        h1 = hm + nn(inner.astype(BF), wdown_ref[...])
        z1 = norm(h1, gain_ref[1, 0:1]).astype(F32)
        for w in range(cols):
            part = slice(w * tokens, (w + 1) * tokens)
            h1_ref[i, :, w, :, :] = h1[part].reshape(WIN, WIN, width)
            z1_ref[i, :, w, :, :] = z1[part].reshape(WIN, WIN, width)
        stage.emit_part(i, z1_ref, h1_ref)
        return 0

    lax.fori_loop(0, rows, body, 0)
    top_ref[...] = z1_ref[0, 0:SHIFT, :, :, :].astype(BF)
    left_ref[...] = z1_ref[:, :, 0, 0:SHIFT, :].astype(BF)
    corner_ref[...] = z1_ref[0, 0:SHIFT, 0, 0:SHIFT, :].astype(BF)


def first_block(order, state5, we, gains, wqkv, wproj, scale, wup, wdown):
    wr, _, wc, _, _ = state5.shape
    width = we.shape[1]
    tokens = wr * wc * WIN * WIN
    chunk = wc * WIN * WIN
    sh = jax.ShapeDtypeStruct
    outs = (
        sh((SHIFT, wc, WIN, width), BF),
        sh((wr, WIN, SHIFT, width), BF),
        sh((SHIFT, SHIFT, width), BF),
        sh((wr, WIN, wc, WIN, width), F32),
        sh((wr, WIN, wc, WIN, width), F32),
        sh((tokens, width), F32),
        sh((tokens, width), F32),
        sh((tokens, 3 * width), BF),
        sh((tokens, wup.shape[2]), BF),
    )
    return staged(
        first_kernel,
        (scale, order, state5, we, gains, wqkv, wproj, wup, wdown),
        outs,
        [
            pltpu.VMEM(state5.shape, F32),
            pltpu.VMEM((width, width), BF),
            pltpu.VMEM((LANES * HEADS // width * WIN * WIN, LANES), BF),
            pltpu.VMEM((chunk, HEADS * WIN * WIN), BF),
            pltpu.VMEM((chunk, width), F32),
            pltpu.SemaphoreType.DMA((wr,)),
        ],
        2e9,
        smem=(0,),
        raw=(1, 2),
        early=load_state,
        layer={5: 0, 6: 0, 7: 0, 8: 0},
    )


def fill_ahead(pad_ref, own, right_ref, below_ref, corner_ref):
    rows, cols, _ = own.shape
    pad_ref[0:rows, 0:cols, :] = own
    pad_ref[0:rows, cols : cols + SHIFT, :] = right_ref[...].astype(F32)
    pad_ref[rows : rows + SHIFT, 0:cols, :] = below_ref[...].astype(F32)
    pad_ref[rows : rows + SHIFT, cols : cols + SHIFT, :] = corner_ref[...].astype(F32)


def rolled_window(pad_ref, i, w):
    block = pad_ref[
        pl.ds(i * WIN + SHIFT, WIN), SHIFT + w * WIN : SHIFT + (w + 1) * WIN, :
    ]
    return block.reshape(WIN * WIN, block.shape[2])


def emit_behind(out_ref, low_ref, east_ref, corner_ref):
    rows, cols, _ = out_ref.shape
    low_ref[...] = out_ref[rows - SHIFT : rows, :, :].astype(BF)
    east_ref[...] = out_ref[:, cols - SHIFT : cols, :].astype(BF)
    corner_ref[...] = out_ref[rows - SHIFT : rows, cols - SHIFT : cols, :].astype(BF)


def shifted_kernel(
    total_rows, stage, start_ref, scale_ref, z1_ref, right_ref, below_ref, corner_ref, wqkv_ref,
    wproj_ref, ans_ref, low_ref, east_ref, last_ref, qkv_ref,
    pad_ref, ones_ref, mask_ref, e_ref, o_ref,
):
    rows, cols, width = z1_ref.shape
    wr, wc = rows // WIN, cols // WIN
    tokens = WIN * WIN
    chunk = wc * tokens
    ones_ref[...] = head_ones(width, width // HEADS)
    mask_ref[...] = head_stack(tokens, width // HEADS)
    scale = scale_lanes(scale_ref, 1, width)
    stage.need(z1_ref, right_ref, below_ref, corner_ref)
    fill_ahead(pad_ref, z1_ref[...], right_ref, below_ref, corner_ref)
    threshold = total_rows - SHIFT - start_ref[0]

    def body(i, _):
        z = jnp.concatenate([rolled_window(pad_ref, i, w).astype(BF) for w in range(wc)], axis=0)
        stage.need_at(i == 0, wqkv_ref, wproj_ref)
        qkv = nn(z, wqkv_ref[...]).astype(BF)
        here = pl.ds(pl.multiple_of(i * chunk, chunk), chunk)
        qkv_ref[here, :] = qkv
        stage.emit_part(here, qkv_ref)
        allowed = side_mask(i, threshold, tokens)
        mixed = attention_chunk(qkv, scale, ones_ref, mask_ref, allowed, e_ref, o_ref, wc, tokens)
        answer = nn(mixed, wproj_ref[...]).astype(BF).astype(F32)
        for w in range(wc):
            ans_ref[pl.ds(i * WIN, WIN), w * WIN : (w + 1) * WIN, :] = answer[
                w * tokens : (w + 1) * tokens
            ].reshape(WIN, WIN, width)
        stage.emit_part(pl.ds(i * WIN, WIN), ans_ref)
        return 0

    lax.fori_loop(0, wr, body, 0)
    emit_behind(ans_ref, low_ref, east_ref, last_ref)


def behind_shapes(rows, cols, width):
    sh = jax.ShapeDtypeStruct
    return (
        sh((rows, cols, width), F32),
        sh((SHIFT, cols, width), BF),
        sh((rows, SHIFT, width), BF),
        sh((SHIFT, SHIFT, width), BF),
    )


def shifted_forward(start, z1, right, below, corner, wqkv, wproj, scale, total_rows):
    rows, cols, width = z1.shape
    tokens = rows * cols
    chunk = cols * WIN
    outs = behind_shapes(rows, cols, width) + (jax.ShapeDtypeStruct((tokens, 3 * width), BF),)
    return staged(
        functools.partial(shifted_kernel, total_rows),
        (start, scale, z1, right, below, corner, wqkv, wproj),
        outs,
        [
            pltpu.VMEM((rows + SHIFT, cols + WIN, width), F32),
            pltpu.VMEM((width, width), BF),
            pltpu.VMEM((LANES * HEADS // width * WIN * WIN, LANES), BF),
            pltpu.VMEM((chunk, HEADS * WIN * WIN), BF),
            pltpu.VMEM((chunk, width), F32),
        ],
        1e9,
        smem=(0, 1),
        vmem=(3, 4, 5),
        layer={6: 1, 7: 1},
    )


def fill_behind(pad_ref, own, above_ref, west_ref, corner_ref):
    rows, cols, _ = own.shape
    pad_ref[SHIFT : SHIFT + rows, SHIFT : SHIFT + cols, :] = own
    pad_ref[0:SHIFT, SHIFT : SHIFT + cols, :] = above_ref[...].astype(F32)
    pad_ref[SHIFT : SHIFT + rows, 0:SHIFT, :] = west_ref[...].astype(F32)
    pad_ref[0:SHIFT, 0:SHIFT, :] = corner_ref[...].astype(F32)


def group_jobs(cnt_smem, offset, size, group, body):
    devices = cnt_smem.shape[0]

    def each(d, _):
        valid = cnt_smem[d, 0] - offset
        for g in range(0, size, group):

            @pl.when(valid > g)
            def _():
                body(d, offset + g, pl.multiple_of(d * size + g, group))

        return 0

    lax.fori_loop(0, devices, each, 0)


def gather_part(table_ref, found_ref, idx_smem, cnt_smem, offset, size, group):
    def body(d, slot, row):
        for u in range(group):
            found_ref[pl.ds(row + u, 1), :] = table_ref[pl.ds(idx_smem[d, slot + u], 1), :]

    group_jobs(cnt_smem, offset, size, group, body)


def scatter_part(table_ref, found_ref, idx_smem, cnt_smem, dup_smem, offset, size, group):
    def body(d, slot, row):
        @pl.when(dup_smem[d, slot] == 0)
        def _():
            spots = [idx_smem[d, slot + u] for u in range(group)]
            sums = [
                table_ref[pl.ds(spots[u], 1), :] + found_ref[pl.ds(row + u, 1), :]
                for u in range(group)
            ]
            for u in range(group):
                table_ref[pl.ds(spots[u], 1), :] = sums[u]

        @pl.when(dup_smem[d, slot] != 0)
        def _():
            def one(u, _):
                spot = pl.ds(idx_smem[d, slot + u], 1)
                table_ref[spot, :] = table_ref[spot, :] + found_ref[pl.ds(row + u, 1), :]
                return 0

            lax.fori_loop(0, group, one, 0)

    group_jobs(cnt_smem, offset, size, group, body)


def radiance_part(found_ref, obs_ref, mixed_ref, w1_ref, size):
    devices, _, channels = obs_ref.shape
    batch = min(devices, max(1, 512 // size))

    def body(i, _):
        here = pl.ds(pl.multiple_of(i * batch * size, batch * size), batch * size)
        y = obs_ref[pl.ds(i * batch, batch), 0:size, :].astype(F32)
        y = y.reshape(batch * size, channels)
        t = jnp.tanh(nn(found_ref[here, :].astype(BF), w1_ref[...].astype(BF)))
        pulled = (nn(t.astype(BF), mixed_ref[...]) - y) * (1.0 - t * t)
        found_ref[here, :] = nt(pulled.astype(BF), w1_ref[...].astype(BF))
        return 0

    lax.fori_loop(0, devices // batch, body, 0)


def spread(table_ref, moved_ref, i, step, tokens):
    for s in range(PIX):
        there = pl.ds(pl.multiple_of(s * tokens + i * step, WIN), step)
        moved_ref[:, s * VARS : (s + 1) * VARS] = table_ref[there, 0:VARS]


def forecast_kernel(
    parts, group, stage, obs1_ref, h1_ref, ans_ref, above_ref, west_ref, corner_ref, gain_ref,
    wup_ref, wdown_ref, whead_ref, state_ref, w1_in_ref, mixed_ref, obs2_ref, back_ref, inv_ref,
    h2_ref, gp_ref, prior_ref, found3_ref, idx_ref, cnt_ref, dup_ref, pulled_ref, w1_ref,
    pad_ref, table_ref, moved_ref, found1_ref, found2_ref, idx_smem, cnt_smem, dup_smem, sems,
):
    rows, cols, width = h1_ref.shape
    devices = obs1_ref.shape[0]
    tokens = rows * cols
    step = tokens // 2

    stage.need(obs1_ref)
    codes = obs1_ref[:, parts[0] : parts[0] + EXTRA, :].astype(F32)[:, 0, :]
    high = codes[:, :LANES].astype(jnp.int32)
    low = codes[:, LANES : 2 * LANES].astype(jnp.int32)
    point = jnp.where(high > 0, (high - 1) * LANES + low, 0)
    lane = lax.broadcasted_iota(jnp.int32, (devices, LANES), 1)
    idx = jnp.where(
        high > 0, (point % PIX) * tokens + point // PIX, PIX * tokens + lane % group
    )
    idx_ref[...] = idx
    cnt_ref[...] = jnp.broadcast_to(
        jnp.sum(jnp.where(high > 0, 1.0, 0.0), 1, keepdims=True), (devices, LANES)
    ).astype(jnp.int32)
    same = jnp.zeros((devices, LANES), jnp.int32)
    for s in range(1, group):
        hit = (pltpu.roll(idx, s, 1) == idx) & (lane % group >= s)
        same = jnp.maximum(same, jnp.where(hit, 1, 0))
    s = group // 2
    while s:
        same = jnp.maximum(same, pltpu.roll(same, LANES - s, 1))
        s //= 2
    dup_ref[...] = same
    copies = [
        pltpu.make_async_copy(a, b, sems.at[n])
        for n, (a, b) in enumerate(
            ((idx_ref, idx_smem), (cnt_ref, cnt_smem), (dup_ref, dup_smem))
        )
    ]
    for copy in copies:
        copy.start()
    stage.need(h1_ref, ans_ref, above_ref, west_ref, corner_ref)
    fill_behind(pad_ref, ans_ref[...], above_ref, west_ref, corner_ref)
    h2_ref[...] = (h1_ref[...] + pad_ref[0:rows, 0:cols, :]).reshape(tokens, width)
    table_ref[PIX * tokens :, :] = jnp.zeros((group, LANES), F32)
    blank = jnp.zeros((step, LANES - VARS), F32)
    stage.need(gain_ref, wup_ref, wdown_ref)

    def forward(i, _):
        here = pl.ds(pl.multiple_of(i * step, step), step)
        h2 = h2_ref[here, :]
        inner, slope = gelu_parts(nn(norm(h2, gain_ref[1, 1:2]), wup_ref[...]))
        gp_ref[here, :] = slope.astype(BF)
        h3 = (h2 + nn(inner.astype(BF), wdown_ref[...])).astype(BF)
        stage.need_at(i == 0, whead_ref, state_ref)
        moved = state_ref[here, :] + nt(h3, whead_ref[...])
        for s in range(PIX):
            there = pl.ds(pl.multiple_of(s * tokens + i * step, WIN), step)
            table_ref[there, :] = jnp.concatenate(
                [moved[:, s * VARS : (s + 1) * VARS], blank], axis=1
            )
        return 0

    lax.fori_loop(0, 2, forward, 0)
    stage.emit(h2_ref, gp_ref, idx_ref, cnt_ref, dup_ref)
    stage.need(back_ref, inv_ref, w1_in_ref, mixed_ref, obs2_ref)
    w1_ref[...] = jnp.zeros_like(w1_ref)
    w1_ref[0:VARS, :] = w1_in_ref[...]
    w1_ref[...] = w1_ref[...].astype(BF).astype(F32)
    for copy in copies:
        copy.wait()
    offsets = (0, parts[0], parts[0] + parts[1])
    founds = (found1_ref, found2_ref, found3_ref)
    for offset, size, found in zip(offsets, parts, founds):
        gather_part(table_ref, found, idx_smem, cnt_smem, offset, size, group)
    stage.emit(found3_ref)
    table_ref[...] = jnp.zeros_like(table_ref)
    radiance_part(found1_ref, obs1_ref, mixed_ref, w1_ref, parts[0])
    scatter_part(table_ref, found1_ref, idx_smem, cnt_smem, dup_smem, 0, parts[0], group)
    radiance_part(found2_ref, obs2_ref, mixed_ref, w1_ref, parts[1])
    scatter_part(table_ref, found2_ref, idx_smem, cnt_smem, dup_smem, parts[0], parts[1], group)

    def collect(i, _):
        here = pl.ds(pl.multiple_of(i * step, step), step)
        spread(table_ref, moved_ref, i, step, tokens)
        moved = moved_ref[...]
        prior_ref[here, :] = moved + inv_ref[...].reshape(1, -1) * (state_ref[here, :] - back_ref[here, :])
        stage.emit_part(here, prior_ref)
        pulled_ref[here, :] = nn(moved.astype(BF), whead_ref[...])
        stage.emit_part(here, pulled_ref)
        return 0

    lax.fori_loop(0, 2, collect, 0)


def forecast(
    h1, ans, above, west, corner, state, background, inv, obs1, obs2, mixed, gains, wup, wdown,
    whead, w1, parts, group,
):
    rows, cols, width = h1.shape
    tokens = rows * cols
    devices = obs1.shape[0]
    sh = jax.ShapeDtypeStruct
    outs = (
        sh((tokens, width), F32),
        sh((tokens, wup.shape[2]), BF),
        sh(state.shape, F32),
        sh((devices * parts[2], LANES), F32),
        sh((devices, LANES), jnp.int32),
        sh((devices, LANES), jnp.int32),
        sh((devices, LANES), jnp.int32),
        sh((tokens, width), F32),
        sh((LANES, w1.shape[1]), F32),
    )
    return staged(
        functools.partial(forecast_kernel, parts, group),
        (
            obs1, h1, ans, above, west, corner, gains, wup, wdown, whead, state, w1, mixed, obs2,
            background, inv,
        ),
        outs,
        [
            pltpu.VMEM((rows + SHIFT, cols + WIN, width), F32),
            pltpu.VMEM((PIX * tokens + group, LANES), F32),
            pltpu.VMEM((tokens // 2, state.shape[1]), F32),
            pltpu.VMEM((devices * parts[0], LANES), F32),
            pltpu.VMEM((devices * parts[1], LANES), F32),
        ]
        + [pltpu.SMEM((devices, LANES), jnp.int32)] * 3
        + [pltpu.SemaphoreType.DMA((3,))],
        3e9,
        vmem=(0, 3, 4, 5, 13),
        layer={7: 1, 8: 1},
    )


def adjoint_kernel(
    parts, group, stage, idx_smem, cnt_smem, dup_smem, w1_ref, mixed_ref, work_ref, obs3_ref,
    whead_ref, pulled_ref, prior_ref, wdown_ref, gp_ref, wup_ref, h2_ref, gain_ref,
    top_ref, left_ref, edge_ref, third_ref, out_ref, table_ref, moved_ref,
):
    rows, cols, width = third_ref.shape
    tokens = rows * cols
    step = tokens // 2
    table_ref[...] = jnp.zeros_like(table_ref)
    stage.need(idx_smem, cnt_smem, dup_smem, w1_ref, mixed_ref, work_ref, obs3_ref)
    radiance_part(work_ref, obs3_ref, mixed_ref, w1_ref, parts[2])
    scatter_part(
        table_ref, work_ref, idx_smem, cnt_smem, dup_smem, parts[0] + parts[1], parts[2], group
    )
    stage.need(whead_ref, pulled_ref, prior_ref, wdown_ref, gp_ref, wup_ref, h2_ref, gain_ref)
    half = rows // 2

    def backward(i, _):
        here = pl.ds(pl.multiple_of(i * step, step), step)
        spread(table_ref, moved_ref, i, step, tokens)
        moved = moved_ref[...]
        out_ref[here, :] = moved + prior_ref[here, :]
        stage.emit_part(here, out_ref)
        grad = (pulled_ref[here, :] + nn(moved.astype(BF), whead_ref[...])).astype(BF)
        d_inner = nt(grad, wdown_ref[...]) * gp_ref[here, :].astype(F32)
        d_normed = nt(d_inner.astype(BF), wup_ref[...])
        third = grad.astype(F32) + norm_back(h2_ref[here, :], gain_ref[1, 1:2], d_normed)
        third_ref[pl.ds(i * half, half), :, :] = third.reshape(half, cols, width)
        stage.emit_part(pl.ds(i * half, half), third_ref)
        return 0

    lax.fori_loop(0, 2, backward, 0)
    top_ref[...] = third_ref[0:SHIFT, :, :].astype(BF)
    left_ref[...] = third_ref[:, 0:SHIFT, :].astype(BF)
    edge_ref[...] = third_ref[0:SHIFT, 0:SHIFT, :].astype(BF)


def adjoint(
    idx, cnt, dup, found, obs3, mixed, w1, h2, gp, gains, wup, wdown, whead, prior, pulled, parts,
    group, rows, cols,
):
    width = h2.shape[1]
    third, top, left, edge = behind_shapes(rows, cols, width)
    outs = (top, left, edge, third, jax.ShapeDtypeStruct(prior.shape, F32))
    return staged(
        functools.partial(adjoint_kernel, parts, group),
        (idx, cnt, dup, w1, mixed, found, obs3, whead, pulled, prior, wdown, gp, wup, h2, gains),
        outs,
        [
            pltpu.VMEM((PIX * rows * cols + group, LANES), F32),
            pltpu.VMEM((prior.shape[0] // 2, prior.shape[1]), F32),
        ],
        2e9,
        scalars=(0, 1, 2),
        vmem=(6,),
        layer={10: 1, 12: 1},
    )


def shifted_back_kernel(
    total_rows, stage, start_ref, scale_ref, third_ref, right_ref, below_ref, corner_ref,
    wproj_ref, qkv_ref, wqkv_ref, dz_ref, low_ref, east_ref, last_ref,
    pad_ref, ones_ref, mask_ref, dq_ref, dk_ref, dv_ref,
):
    rows, cols, width = third_ref.shape
    wr, wc = rows // WIN, cols // WIN
    tokens = WIN * WIN
    chunk = wc * tokens
    ones_ref[...] = head_ones(width, width // HEADS)
    mask_ref[...] = head_stack(tokens, width // HEADS)
    scale = scale_lanes(scale_ref, 1, width)
    stage.need(third_ref, right_ref, below_ref, corner_ref)
    fill_ahead(pad_ref, third_ref[...], right_ref, below_ref, corner_ref)
    threshold = total_rows - SHIFT - start_ref[0]

    def body(i, _):
        d_answer = jnp.concatenate(
            [rolled_window(pad_ref, i, w).astype(BF) for w in range(wc)], axis=0
        )
        stage.need_at(i == 0, wproj_ref, qkv_ref, wqkv_ref)
        d_out = nt(d_answer, wproj_ref[...]).astype(BF)
        allowed = side_mask(i, threshold, tokens)
        qkv = qkv_ref[pl.ds(pl.multiple_of(i * chunk, chunk), chunk), :]
        d_qkv = attention_chunk_back(
            qkv, d_out, scale, ones_ref, mask_ref, allowed,
            dq_ref, dk_ref, dv_ref, wc, tokens,
        )
        dz = nt(d_qkv, wqkv_ref[...]).astype(BF).astype(F32)
        for w in range(wc):
            dz_ref[pl.ds(i * WIN, WIN), w * WIN : (w + 1) * WIN, :] = dz[
                w * tokens : (w + 1) * tokens
            ].reshape(WIN, WIN, width)
        stage.emit_part(pl.ds(i * WIN, WIN), dz_ref)
        return 0

    lax.fori_loop(0, wr, body, 0)
    emit_behind(dz_ref, low_ref, east_ref, last_ref)


def shifted_backward(start, third, right, below, corner, qkv, wqkv, wproj, scale, total_rows):
    rows, cols, width = third.shape
    chunk = cols * WIN
    outs = behind_shapes(rows, cols, width)
    return staged(
        functools.partial(shifted_back_kernel, total_rows),
        (start, scale, third, right, below, corner, wproj, qkv, wqkv),
        outs,
        [
            pltpu.VMEM((rows + SHIFT, cols + WIN, width), F32),
            pltpu.VMEM((width, width), BF),
            pltpu.VMEM((LANES * HEADS // width * WIN * WIN, LANES), BF),
        ]
        + [pltpu.VMEM((chunk, width), F32)] * 3,
        1e9,
        smem=(0, 1),
        vmem=(3, 4, 5, 6, 7, 8),
        layer={6: 1, 8: 1},
    )


def last_kernel(
    stage, scale_ref, partial_hbm, dz_ref, above_ref, west_ref, corner_ref, third_ref, h1_ref,
    gain_ref, wdown_ref, gp_ref, wup_ref, hm_ref, wproj_ref, qkv_ref, wqkv_ref, h0_ref, we_ref,
    out_hbm,
    pad_ref, ones_ref, mask_ref, dq_ref, dk_ref, dv_ref, out_ref, in_sems, out_sems,
):
    rows, cols, width = dz_ref.shape
    wr, wc = rows // WIN, cols // WIN
    tokens = WIN * WIN
    chunk = wc * tokens

    def rows_of(ref, i):
        return ref.at[pl.ds(i * WIN, WIN)]

    ones_ref[...] = head_ones(width, width // HEADS)
    mask_ref[...] = head_stack(tokens, width // HEADS)
    scale = scale_lanes(scale_ref, 0, width)
    for i in range(wr):
        pltpu.make_async_copy(rows_of(partial_hbm, i), rows_of(out_ref, i), in_sems.at[i]).start()
    stage.need(dz_ref, above_ref, west_ref, corner_ref)
    fill_behind(pad_ref, dz_ref[...], above_ref, west_ref, corner_ref)

    def body(i, _):
        here = pl.ds(pl.multiple_of(i * chunk, chunk), chunk)
        band = pl.ds(i * WIN, WIN)

        def take(ref):
            return jnp.concatenate(
                [
                    ref[band, w * WIN : (w + 1) * WIN, :].reshape(tokens, width)
                    for w in range(wc)
                ],
                axis=0,
            )

        stage.need_at(i == 0, third_ref, h1_ref, gain_ref, wdown_ref, gp_ref, wup_ref)
        second = take(third_ref) + norm_back(take(h1_ref), gain_ref[1, 0:1], take(pad_ref))
        d_inner = nt(second.astype(BF), wdown_ref[...]) * gp_ref[here, :].astype(F32)
        d_normed = nt(d_inner.astype(BF), wup_ref[...])
        stage.need_at(i == 0, hm_ref, wproj_ref, qkv_ref, wqkv_ref, h0_ref, we_ref)
        d_hm = second + norm_back(hm_ref[here, :], gain_ref[0, 1:2], d_normed)
        d_out = nt(d_hm.astype(BF), wproj_ref[...]).astype(BF)
        d_qkv = attention_chunk_back(
            qkv_ref[here, :], d_out, scale, ones_ref, mask_ref, None,
            dq_ref, dk_ref, dv_ref, wc, tokens,
        )
        dz = nt(d_qkv, wqkv_ref[...])
        d_h0 = (d_hm + norm_back(h0_ref[here, :], gain_ref[0, 0:1], dz)).astype(BF)
        pltpu.make_async_copy(rows_of(partial_hbm, i), rows_of(out_ref, i), in_sems.at[i]).wait()
        for w in range(wc):
            grad = nt(d_h0[w * tokens : (w + 1) * tokens], we_ref[...])
            grad = grad.reshape(WIN, WIN, grad.shape[1])
            spot = (band, slice(w * WIN, (w + 1) * WIN), slice(None))
            out_ref[spot] = grad + out_ref[spot]
        pltpu.make_async_copy(rows_of(out_ref, i), rows_of(out_hbm, i), out_sems.at[i]).start()
        return 0

    lax.fori_loop(0, wr, body, 0)
    for i in range(wr):
        pltpu.make_async_copy(rows_of(out_ref, i), rows_of(out_hbm, i), out_sems.at[i]).wait()


def last_block(
    third, dz, above, west, corner, h1, h0, hm, qkv, gp, we, gains, wqkv, wproj, scale,
    wup, wdown, partial,
):
    rows, cols, width = dz.shape
    chunk = cols * WIN
    (result,) = staged(
        last_kernel,
        (
            scale, partial, dz, above, west, corner, third, h1, gains, wdown, gp, wup, hm, wproj,
            qkv, wqkv, h0, we,
        ),
        (jax.ShapeDtypeStruct(partial.shape, F32),),
        [
            pltpu.VMEM((rows + SHIFT, cols + WIN, width), F32),
            pltpu.VMEM((width, width), BF),
            pltpu.VMEM((LANES * HEADS // width * WIN * WIN, LANES), BF),
        ]
        + [pltpu.VMEM((chunk, width), F32)] * 3
        + [
            pltpu.VMEM(partial.shape, F32),
            pltpu.SemaphoreType.DMA((rows // WIN,)),
            pltpu.SemaphoreType.DMA((rows // WIN,)),
        ],
        2e9,
        smem=(0,),
        raw=(1,),
        raw_outs=(0,),
        vmem=(3, 4, 5, 7, 8, 9, 10, 11, 12, 13, 14, 15, 16, 17),
        layer={9: 0, 11: 0, 13: 0, 15: 0},
    )
    return result


def neighbour(x, by_lat, by_lon):
    lat, lon = lax.axis_size("lat"), lax.axis_size("lon")
    pairs = [
        (a * lon + b, ((a + by_lat) % lat) * lon + (b + by_lon) % lon)
        for a in range(lat)
        for b in range(lon)
    ]
    return lax.ppermute(x, ("lat", "lon"), pairs)


def exchange(x):
    return lax.all_to_all(x, ("lat", "lon"), split_axis=0, concat_axis=0, tiled=True)


def local(
    state,
    background,
    inv_background,
    w_embed,
    norm_gain,
    w_qkv,
    w_proj,
    head_scale,
    w_up,
    w_down,
    w_head,
    w_obs1,
    w_obs2,
    r_inverse,
    obs_values,
    obs_owner,
    obs_point,
    obs_count,
):
    rows, cols, patch_values = state.shape
    width = w_embed.shape[1]
    total_rows = rows * lax.axis_size("lat")
    row_start = (lax.axis_index("lat") * rows).astype(jnp.int32).reshape(1)
    devices = lax.axis_size("lat") * lax.axis_size("lon")
    slots = obs_values.shape[0]
    cap = 2 * slots // devices

    parts, group = split(cap)

    send1, send2, send3, mixed = route(
        obs_owner.reshape(1, slots), obs_point.reshape(1, slots), obs_count, obs_values,
        r_inverse, w_obs2, devices, parts,
    )
    obs1 = exchange(send1)
    state5 = state.reshape(rows // WIN, WIN, cols // WIN, WIN, patch_values)
    top, left, corner, z1, h1, h0, hm, qkv0, gp0 = first_block(
        mixed, state5, w_embed, norm_gain, w_qkv, w_proj, head_scale, w_up, w_down
    )
    z1 = z1.reshape(rows, cols, width)
    h1 = h1.reshape(rows, cols, width)
    below = neighbour(top.reshape(SHIFT, cols, width), -1, 0)
    right = neighbour(left.reshape(rows, SHIFT, width), 0, -1)
    corner = neighbour(corner, -1, -1)
    obs1, send2 = lax.optimization_barrier((obs1, send2))
    obs2 = exchange(send2)
    answer, low, east, last, qkv1 = shifted_forward(
        row_start, z1, right, below, corner, w_qkv, w_proj, head_scale, total_rows
    )
    above = neighbour(low, 1, 0)
    west = neighbour(east, 0, 1)
    last = neighbour(last, 1, 1)
    obs2, send3 = lax.optimization_barrier((obs2, send3))
    obs3 = exchange(send3)
    flat = (rows * cols, patch_values)
    h2, gp1, prior, found, idx, cnt, dup, pulled, w1 = forecast(
        h1, answer, above, west, last, state.reshape(flat), background.reshape(flat),
        inv_background, obs1, obs2, mixed, norm_gain, w_up, w_down, w_head.T,
        w_obs1, parts, group,
    )
    top, left, corner, third, partial = adjoint(
        idx, cnt, dup, found, obs3, mixed, w1, h2, gp1, norm_gain, w_up, w_down, w_head.T, prior,
        pulled,
        parts, group, rows, cols,
    )
    below = neighbour(top, -1, 0)
    right = neighbour(left, 0, -1)
    corner = neighbour(corner, -1, -1)
    dz, low, east, last = shifted_backward(
        row_start, third, right, below, corner, qkv1, w_qkv, w_proj, head_scale, total_rows
    )
    above = neighbour(low, 1, 0)
    west = neighbour(east, 0, 1)
    last = neighbour(last, 1, 1)
    return last_block(
        third, dz, above, west, last, h1, h0, hm, qkv0, gp0, w_embed, norm_gain, w_qkv, w_proj,
        head_scale, w_up, w_down, partial.reshape(state.shape),
    )


def solution(mesh):
    placed = (
        P("lat", "lon", None),
        P("lat", "lon", None),
        P(),
        P(),
        P(),
        P(),
        P(),
        P(),
        P(),
        P(),
        P(),
        P(),
        P(),
        P(),
        P(("lat", "lon"), None),
        P(("lat", "lon"), None),
        P(("lat", "lon")),
        P(("lat", "lon")),
    )

    return jax.shard_map(
        local, mesh=mesh, in_specs=placed, out_specs=P("lat", "lon", None), check_vma=False
    )
```

profile of v0, /device:TPU:0, one launch (start us, length us, event | category | flops | bytes accessed | tf_op | source)
XLA Modules:
  0.0 166.1 jit_solution(1738881431767529801)
XLA Ops:
  0.7 7.3 %shard_map.172 = (bf16[32,40,256]{2,1,0:T(8,128)(2,1)}, bf16[32,32,256]{2,1,0:T(8,128)(2,1)}, bf16[32,64,256]{2,1,0:T(8,128)(2,1)}, bf16[256,256]{1,0:T(8,128)(2,1)}) custom-call(s32[1]{0:T(128)S(6)} %copy.19.refs_0_, s32[1,2048]{1,0:T(1,128)} %bitcast.22, s32[1,2048]{1,0:T(1,128)} %bitcast.23, f32[256,256]{1,0:T(8,128)} %refs_3_.2, f32[256,256]{1,0:T(8,128)} %refs_4_.2, ...), custom_call_target="tpu_custom_call" | custom-call | flops 1000000000 | bytes 8388608 | tf_op jit(solution)/shard_map/pallas_call | solution.py:137
  7.9 26.4 %all_to_all.15.refs_0_ = bf16[32,40,256]{2,1,0:T(8,128)(2,1)S(1)} all-to-all(bf16[32,40,256]{2,1,0:T(8,128)(2,1)} %get-tuple-element.45), channel_id=1, replica_groups=mesh['lat'=4,'lon'=8] {'lat','lon'}, dimensions={0} | all-to-all | bytes 1310720 | tf_op jit(solution)/shard_map/all_to_all | solution.py:1064
  34.3 18.8 %all_to_all.16.refs_13_ = bf16[32,32,256]{2,1,0:T(8,128)(2,1)S(1)} all-to-all(bf16[32,32,256]{2,1,0:T(8,128)(2,1)} %get-tuple-element.58), channel_id=1, replica_groups=mesh['lat'=4,'lon'=8] {'lat','lon'}, dimensions={0} | all-to-all | bytes 1048576 | tf_op jit(solution)/shard_map/all_to_all | solution.py:1064
  53.2 2.6 %all-to-all-start.2 = ((bf16[32,64,256]{2,1,0:T(8,128)(2,1)}), bf16[32,64,256]{2,1,0:T(8,128)(2,1)S(1)}, u32[]{:S(2)}, u32[]{:S(2)}) async-start(bf16[32,64,256]{2,1,0:T(8,128)(2,1)} %get-tuple-element.66), calls=%async_computation.2 | async-start | bytes 2097152 | tf_op jit(solution)/shard_map/all_to_all | solution.py:1064
  55.8 0.0 copy-done.11
  55.8 12.3 %shard_map.173 = (bf16[4,6,8,256]{3,2,1,0:T(8,128)(2,1)}, bf16[2,8,4,256]{3,2,1,0:T(4,128)(2,1)}, bf16[4,4,256]{2,1,0:T(4,128)(2,1)}, f32[2,8,6,8,256]{4,3,2,1,0...) custom-call(f32[2,8]{1,0:T(2,128)S(1)} %copy-done.11, ...), custom_call_target="tpu_custom_call" | custom-call | flops 2000000000 | bytes 8388608 | tf_op jit(solution)/shard_map/pallas_call | solution.py:137
  68.2 2.6 %collective-permute-start.1 = (bf16[4,48,256]{2,1,0:T(8,128)(2,1)}, bf16[4,48,256]{2,1,0:T(8,128)(2,1)S(1)}, u32[]{:S(2)}, u32[]{:S(2)}) collective-permute-start(bf16[4,48,256]{2,1,0:T(8,128)(2,1)} %bitcast.20), channel_id=1, source_target_pairs={{0,24},{1,25},{2,26},{3,27},{4,28},{5,29},{6,30},{7,31},{8,0},{9,1... | collective-permute-start | bytes 294920 | tf_op jit(solution)/shard_map/ppermute | solution.py:1060
  70.8 2.9 %collective-permute-start = (bf16[16,4,256]{2,1,0:T(4,128)(2,1)}, bf16[16,4,256]{2,1,0:T(4,128)(2,1)S(1)}, u32[]{:S(2)}, u32[]{:S(2)}) collective-permute-start(bf16[16,4,256]{2,1,0:T(4,128)(2,1)} %bitcast.21), channel_id=1, source_target_pairs={{0,7},{1,0},{2,1},{3,2},{4,3},{5,4},{6,5},{7,6},{8,15},{9,8},{10,9... | collective-permute-start | bytes 98312 | tf_op jit(solution)/shard_map/ppermute | solution.py:1060
  73.7 0.6 collective-permute-start.2
  74.4 2.7 %collective-permute-done.2.refs_5_ = bf16[4,4,256]{2,1,0:T(4,128)(2,1)S(1)} collective-permute-done((bf16[4,4,256]{2,1,0:T(4,128)(2,1)}, bf16[4,4,256]{2,1,0:T(4,128)(2,1)S(1)}, u32[]{:S(2)}, u32[]{:S(2)}) %collective-permute-start.2) | collective-permute-done | bytes 8224 | tf_op jit(solution)/shard_map/ppermute | solution.py:1060
  77.0 0.0 collective-permute-done.refs_3_
  77.1 0.0 collective-permute-done.1.refs_4_
  77.1 6.2 %shard_map.174 = (f32[16,48,256]{2,1,0:T(8,128)}, bf16[4,48,256]{2,1,0:T(8,128)(2,1)}, bf16[16,4,256]{2,1,0:T(4,128)(2,1)}, bf16[4,4,256]{2,1,0:T(4,128)(2,1)}, bf16[768,768]{1,0:T(8,128)(2,1)}) custom-call(s32[1]{0:T(128)} %bitcast.4.refs_0_, f32[2,8]{1,0:T(2,128)S(1)} %copy-done.11, f32[16,48,256]{2,1,0:T(8,128)} %bitcast.24, ...), custom_call_target="tpu_custom_call" | custom-call | flops 1000000000 | bytes 8388608 | tf_op jit(solution)/shard_map/pallas_call | solution.py:137
  83.3 1.0 collective-permute-start.3
  84.3 0.0 collective-permute-start.4
  84.3 1.1 collective-permute-start.5
  85.4 5.8 %collective-permute-done.5.refs_5_ = bf16[4,4,256]{2,1,0:T(4,128)(2,1)S(1)} collective-permute-done((bf16[4,4,256]{2,1,0:T(4,128)(2,1)}, bf16[4,4,256]{2,1,0:T(4,128)(2,1)S(1)}, u32[]{:S(2)}, u32[]{:S(2)}) %collective-permute-start.5) | collective-permute-done | bytes 8224 | tf_op jit(solution)/shard_map/ppermute | solution.py:1060
  91.2 0.0 collective-permute-done.4.refs_4_
  91.2 0.0 collective-permute-done.3.refs_3_
  91.2 22.5 %shard_map.175 = (f32[768,256]{1,0:T(8,128)}, bf16[768,1024]{1,0:T(8,128)(2,1)}, f32[768,1104]{1,0:T(8,128)}, f32[2048,128]{1,0:T(8,128)}, s32[32,128]{1,0:T(8,1...) custom-call(bf16[32,40,256]{2,1,0:T(8,128)(2,1)S(1)} %all_to_all.15.refs_0_, ...), custom_call_target="tpu_custom_call" | custom-call | flops 3000000000 | bytes 8388608 | tf_op jit(solution)/shard_map/pallas_call | solution.py:137
  113.7 0.0 all-to-all-done.2.refs_6_
  113.7 0.0 copy-start.5
  113.7 0.0 copy-start.9
  113.7 0.0 copy-start.12
  113.7 0.0 copy-start.3
  113.7 0.0 copy-start.4
  113.8 0.0 copy-start.7
  113.8 0.0 copy-start.8
  113.8 10.1 %shard_map.176 = (bf16[4,48,256]{2,1,0:T(8,128)(2,1)}, bf16[16,4,256]{2,1,0:T(4,128)(2,1)}, bf16[4,4,256]{2,1,0:T(4,128)(2,1)}, f32[16,48,256]{2,1,0:T(8,128)}, f32[768,1104]{1,0:T(8,128)}) custom-call(s32[32,128]{1,0:T(8,128)} %get-tuple-element.61.refs_0_, s32[32,128]{1,0:T(8,128)} %get-tuple-element.62.refs_1_, s32[32,128]{1,0:T(8,128)} %get-tuple-element.63.refs_2_, ...), custom_call_target="tpu_custom_call" | custom-call | flops 2000000000 | bytes 8388608 | tf_op jit(solution)/shard_map/pallas_call | solution.py:137
  123.9 0.0 copy-start
  123.9 0.0 copy-start.1
  123.9 0.0 copy-start.2
  123.9 0.0 copy-start.6
  123.9 0.0 copy-start.10
  124.0 0.1 collective-permute-start.7
  124.0 3.2 %collective-permute-start.6 = (bf16[16,4,256]{2,1,0:T(4,128)(2,1)}, bf16[16,4,256]{2,1,0:T(4,128)(2,1)S(1)}, u32[]{:S(2)}, u32[]{:S(2)}) collective-permute-start(bf16[16,4,256]{2,1,0:T(4,128)(2,1)} %get-tuple-element.73), channel_id=1, source_target_pairs={{0,7},{1,0},{2,1},{3,2},{4,3},{5,4},{6,5},{7,6},{8,15},{9,8},{10,9... | collective-permute-start | bytes 98312 | tf_op jit(solution)/shard_map/ppermute | solution.py:1060
  127.2 0.0 collective-permute-start.8
  127.2 3.3 %collective-permute-done.8.refs_5_ = bf16[4,4,256]{2,1,0:T(4,128)(2,1)S(1)} collective-permute-done((bf16[4,4,256]{2,1,0:T(4,128)(2,1)}, bf16[4,4,256]{2,1,0:T(4,128)(2,1)S(1)}, u32[]{:S(2)}, u32[]{:S(2)}) %collective-permute-start.8) | collective-permute-done | bytes 8224 | tf_op jit(solution)/shard_map/ppermute | solution.py:1060
  130.5 0.0 collective-permute-done.6.refs_3_
  130.5 0.0 collective-permute-done.7.refs_4_
  130.5 8.2 %shard_map.177 = (f32[16,48,256]{2,1,0:T(8,128)}, bf16[4,48,256]{2,1,0:T(8,128)(2,1)}, bf16[16,4,256]{2,1,0:T(4,128)(2,1)}, bf16[4,4,256]{2,1,0:T(4,128)(2,1)}) custom-call(s32[1]{0:T(128)} %bitcast.4.refs_0_, f32[2,8]{1,0:T(2,128)S(1)} %copy-done.11, f32[16,48,256]{2,1,0:T(8,128)} %get-tuple-element.72.refs_2_.refs_6_, ...), custom_call_target="tpu_custom_call" | custom-call | flops 1000000000 | bytes 8388608 | tf_op jit(solution)/shard_map/pallas_call | solution.py:137
  138.7 2.9 %collective-permute-start.9 = (bf16[4,48,256]{2,1,0:T(8,128)(2,1)}, bf16[4,48,256]{2,1,0:T(8,128)(2,1)S(1)}, u32[]{:S(2)}, u32[]{:S(2)}) collective-permute-start(bf16[4,48,256]{2,1,0:T(8,128)(2,1)} %get-tuple-element.78), channel_id=1, source_target_pairs={{0,8},{1,9},{2,10},{3,11},{4,12},{5,13},{6,14},{7,15},{8,16},{9,17... | collective-permute-start | bytes 294920 | tf_op jit(solution)/shard_map/ppermute | solution.py:1060
  141.7 3.2 %collective-permute-start.10 = (bf16[16,4,256]{2,1,0:T(4,128)(2,1)}, bf16[16,4,256]{2,1,0:T(4,128)(2,1)S(1)}, u32[]{:S(2)}, u32[]{:S(2)}) collective-permute-start(bf16[16,4,256]{2,1,0:T(4,128)(2,1)} %get-tuple-element.79), channel_id=1, source_target_pairs={{0,1},{1,2},{2,3},{3,4},{4,5},{5,6},{6,7},{7,0},{8,9},{9,10},{10,1... | collective-permute-start | bytes 98312 | tf_op jit(solution)/shard_map/ppermute | solution.py:1060
  144.9 3.3 %collective-permute-start.11 = (bf16[4,4,256]{2,1,0:T(4,128)(2,1)}, bf16[4,4,256]{2,1,0:T(4,128)(2,1)S(1)}, u32[]{:S(2)}, u32[]{:S(2)}) collective-permute-start(bf16[4,4,256]{2,1,0:T(4,128)(2,1)} %get-tuple-element.80), channel_id=1, source_target_pairs={{0,9},{1,10},{2,11},{3,12},{4,13},{5,14},{6,15},{7,8},{8,17},{9,18... | collective-permute-start | bytes 24584 | tf_op jit(solution)/shard_map/ppermute | solution.py:1060
  148.2 3.6 %collective-permute-done.11.refs_5_ = bf16[4,4,256]{2,1,0:T(4,128)(2,1)S(1)} collective-permute-done((bf16[4,4,256]{2,1,0:T(4,128)(2,1)}, bf16[4,4,256]{2,1,0:T(4,128)(2,1)S(1)}, u32[]{:S(2)}, u32[]{:S(2)}) %collective-permute-start.11) | collective-permute-done | bytes 8224 | tf_op jit(solution)/shard_map/ppermute | solution.py:1060
  151.7 0.0 collective-permute-done.10.refs_4_
  151.7 0.0 collective-permute-done.9.refs_3_
  151.8 14.1 %shard_map.178 = f32[16,48,1104]{2,1,0:T(8,128)} custom-call(f32[2,8]{1,0:T(2,128)S(1)} %copy-done.11, f32[16,48,1104]{2,1,0:T(8,128)} %bitcast.17, f32[16,48,256]{2,1,0:T(8,128)} %get-tuple-element.77.refs_2_, bf16[4,48,256]{2,1,0:T(8,128)(2,1)S(1)} %collective-permute-done.9.refs_3_, bf16[16,4,256]{2,1,0:T(4,128)(2,1)S(1)} %collective-permute-done.10.refs_4_, ...), custom_call_target="tpu_custom_call" | custom-call | flops 2000000000 | bytes 8388608 | tf_op jit(solution)/shard_map/pallas_call | solution.py:137
  (13 shorter events, 0.0 us)
Async XLA Ops:
  0.7 55.2 %copy-start.11 = (f32[2,8]{1,0:T(2,128)S(1)}, f32[2,8]{1,0:T(2,128)}, u32[]{:S(2)}) copy-start(f32[2,8]{1,0:T(2,128)} %refs_0_.4) | copy-start | bytes 196
  53.2 60.5 %all-to-all-start.2 = ((bf16[32,64,256]{2,1,0:T(8,128)(2,1)}), bf16[32,64,256]{2,1,0:T(8,128)(2,1)S(1)}, u32[]{:S(2)}, u32[]{:S(2)}) async-start(bf16[32,64,256]{2,1,0:T(8,128)(2,1)} %get-tuple-element.66), calls=%async_computation.2 | async-start | bytes 2097152 | tf_op jit(solution)/shard_map/all_to_all | solution.py:1064
  68.2 8.9 %collective-permute-start.1 = (bf16[4,48,256]{2,1,0:T(8,128)(2,1)}, bf16[4,48,256]{2,1,0:T(8,128)(2,1)S(1)}, u32[]{:S(2)}, u32[]{:S(2)}) collective-permute-start(bf16[4,48,256]{2,1,0:T(8,128)(2,1)} %bitcast.20), channel_id=1, source_target_pairs={{0,24},{1,25},{2,26},{3,27},{4,28},{5,29},{6,30},{7,31},{8,0},{9,1... | collective-permute-start | bytes 294920 | tf_op jit(solution)/shard_map/ppermute | solution.py:1060
  70.8 6.3 %collective-permute-start = (bf16[16,4,256]{2,1,0:T(4,128)(2,1)}, bf16[16,4,256]{2,1,0:T(4,128)(2,1)S(1)}, u32[]{:S(2)}, u32[]{:S(2)}) collective-permute-start(bf16[16,4,256]{2,1,0:T(4,128)(2,1)} %bitcast.21), channel_id=1, source_target_pairs={{0,7},{1,0},{2,1},{3,2},{4,3},{5,4},{6,5},{7,6},{8,15},{9,8},{10,9... | collective-permute-start | bytes 98312 | tf_op jit(solution)/shard_map/ppermute | solution.py:1060
  73.7 3.3 %collective-permute-start.2 = (bf16[4,4,256]{2,1,0:T(4,128)(2,1)}, bf16[4,4,256]{2,1,0:T(4,128)(2,1)S(1)}, u32[]{:S(2)}, u32[]{:S(2)}) collective-permute-start(bf16[4,4,256]{2,1,0:T(4,128)(2,1)} %get-tuple-element.53), channel_id=1, source_target_pairs={{0,31},{1,24},{2,25},{3,26},{4,27},{5,28},{6,29},{7,30},{8,7},{9,0... | collective-permute-start | bytes 24584 | tf_op jit(solution)/shard_map/ppermute | solution.py:1060
  83.3 7.9 %collective-permute-start.3 = (bf16[4,48,256]{2,1,0:T(8,128)(2,1)}, bf16[4,48,256]{2,1,0:T(8,128)(2,1)S(1)}, u32[]{:S(2)}, u32[]{:S(2)}) collective-permute-start(bf16[4,48,256]{2,1,0:T(8,128)(2,1)} %get-tuple-element.55), channel_id=1, source_target_pairs={{0,8},{1,9},{2,10},{3,11},{4,12},{5,13},{6,14},{7,15},{8,16},{9,17... | collective-permute-start | bytes 294920 | tf_op jit(solution)/shard_map/ppermute | solution.py:1060
  84.3 6.9 %collective-permute-start.4 = (bf16[16,4,256]{2,1,0:T(4,128)(2,1)}, bf16[16,4,256]{2,1,0:T(4,128)(2,1)S(1)}, u32[]{:S(2)}, u32[]{:S(2)}) collective-permute-start(bf16[16,4,256]{2,1,0:T(4,128)(2,1)} %get-tuple-element.56), channel_id=1, source_target_pairs={{0,1},{1,2},{2,3},{3,4},{4,5},{5,6},{6,7},{7,0},{8,9},{9,10},{10,1... | collective-permute-start | bytes 98312 | tf_op jit(solution)/shard_map/ppermute | solution.py:1060
  84.3 6.9 %collective-permute-start.5 = (bf16[4,4,256]{2,1,0:T(4,128)(2,1)}, bf16[4,4,256]{2,1,0:T(4,128)(2,1)S(1)}, u32[]{:S(2)}, u32[]{:S(2)}) collective-permute-start(bf16[4,4,256]{2,1,0:T(4,128)(2,1)} %get-tuple-element.57), channel_id=1, source_target_pairs={{0,9},{1,10},{2,11},{3,12},{4,13},{5,14},{6,15},{7,8},{8,17},{9,18... | collective-permute-start | bytes 24584 | tf_op jit(solution)/shard_map/ppermute | solution.py:1060
  113.7 16.8 %copy-start.5 = (bf16[2,256,768]{2,1,0:T(8,128)(2,1)S(1)}, bf16[2,256,768]{2,1,0:T(8,128)(2,1)}, u32[]{:S(2)}) copy-start(bf16[2,256,768]{2,1,0:T(8,128)(2,1)} %refs_15_.3) | copy-start | bytes 2359300
  113.7 16.8 %copy-start.9 = (bf16[2,256,256]{2,1,0:T(8,128)(2,1)S(1)}, bf16[2,256,256]{2,1,0:T(8,128)(2,1)}, u32[]{:S(2)}) copy-start(bf16[2,256,256]{2,1,0:T(8,128)(2,1)} %refs_13_.1) | copy-start | bytes 786436
  113.7 16.8 %copy-start.12 = (bf16[768,768]{1,0:T(8,128)(2,1)S(1)}, bf16[768,768]{1,0:T(8,128)(2,1)}, u32[]{:S(2)}) copy-start(bf16[768,768]{1,0:T(8,128)(2,1)} %get-tuple-element.76.refs_7_) | copy-start | bytes 3538948
  113.7 38.0 %copy-start.3 = (bf16[768,1024]{1,0:T(8,128)(2,1)S(1)}, bf16[768,1024]{1,0:T(8,128)(2,1)}, u32[]{:S(2)}) copy-start(bf16[768,1024]{1,0:T(8,128)(2,1)} %get-tuple-element.81.refs_10_) | copy-start | bytes 4718596
  113.7 38.0 %copy-start.4 = (bf16[768,768]{1,0:T(8,128)(2,1)S(1)}, bf16[768,768]{1,0:T(8,128)(2,1)}, u32[]{:S(2)}) copy-start(bf16[768,768]{1,0:T(8,128)(2,1)} %get-tuple-element.83.refs_14_) | copy-start | bytes 3538948
  113.8 38.0 %copy-start.7 = (f32[768,256]{1,0:T(8,128)S(1)}, f32[768,256]{1,0:T(8,128)}, u32[]{:S(2)}) copy-start(f32[768,256]{1,0:T(8,128)} %get-tuple-element.82.refs_12_) | copy-start | bytes 2359300
  113.8 38.0 %copy-start.8 = (bf16[1104,256]{1,0:T(8,128)(2,1)S(1)}, bf16[1104,256]{1,0:T(8,128)(2,1)}, u32[]{:S(2)}) copy-start(bf16[1104,256]{1,0:T(8,128)(2,1)} %refs_17_.1) | copy-start | bytes 1695748
  123.9 27.9 %copy-start = (bf16[2,256,1024]{2,1,0:T(8,128)(2,1)S(1)}, bf16[2,256,1024]{2,1,0:T(8,128)(2,1)}, u32[]{:S(2)}) copy-start(bf16[2,256,1024]{2,1,0:T(8,128)(2,1)} %refs_11_.3) | copy-start | bytes 3145732
  123.9 27.9 %copy-start.1 = (bf16[2,1024,256]{2,1,0:T(8,128)(2,1)S(1)}, bf16[2,1024,256]{2,1,0:T(8,128)(2,1)}, u32[]{:S(2)}) copy-start(bf16[2,1024,256]{2,1,0:T(8,128)(2,1)} %refs_9_.1) | copy-start | bytes 3145732
  123.9 27.9 %copy-start.2 = (f32[2,8,6,8,256]{4,3,2,1,0:T(8,128)S(1)}, f32[2,8,6,8,256]{4,3,2,1,0:T(8,128)}, u32[]{:S(2)}) copy-start(f32[2,8,6,8,256]{4,3,2,1,0:T(8,128)} %get-tuple-element.49) | copy-start | bytes 2359300
  123.9 27.9 %copy-start.6 = (f32[768,256]{1,0:T(8,128)S(1)}, f32[768,256]{1,0:T(8,128)}, u32[]{:S(2)}) copy-start(f32[768,256]{1,0:T(8,128)} %get-tuple-element.84.refs_16_) | copy-start | bytes 2359300
  123.9 27.9 %copy-start.10 = (f32[2,2,256]{2,1,0:T(2,128)S(1)}, f32[2,2,256]{2,1,0:T(2,128)}, u32[]{:S(2)}) copy-start(f32[2,2,256]{2,1,0:T(2,128)} %refs_8_.7) | copy-start | bytes 12292
  124.0 6.5 %collective-permute-start.7 = (bf16[4,48,256]{2,1,0:T(8,128)(2,1)}, bf16[4,48,256]{2,1,0:T(8,128)(2,1)S(1)}, u32[]{:S(2)}, u32[]{:S(2)}) collective-permute-start(bf16[4,48,256]{2,1,0:T(8,128)(2,1)} %get-tuple-element.74), channel_id=1, source_target_pairs={{0,24},{1,25},{2,26},{3,27},{4,28},{5,29},{6,30},{7,31},{8,0},{9,1... | collective-permute-start | bytes 294920 | tf_op jit(solution)/shard_map/ppermute | solution.py:1060
  124.0 6.4 %collective-permute-start.6 = (bf16[16,4,256]{2,1,0:T(4,128)(2,1)}, bf16[16,4,256]{2,1,0:T(4,128)(2,1)S(1)}, u32[]{:S(2)}, u32[]{:S(2)}) collective-permute-start(bf16[16,4,256]{2,1,0:T(4,128)(2,1)} %get-tuple-element.73), channel_id=1, source_target_pairs={{0,7},{1,0},{2,1},{3,2},{4,3},{5,4},{6,5},{7,6},{8,15},{9,8},{10,9... | collective-permute-start | bytes 98312 | tf_op jit(solution)/shard_map/ppermute | solution.py:1060
  127.2 3.3 %collective-permute-start.8 = (bf16[4,4,256]{2,1,0:T(4,128)(2,1)}, bf16[4,4,256]{2,1,0:T(4,128)(2,1)S(1)}, u32[]{:S(2)}, u32[]{:S(2)}) collective-permute-start(bf16[4,4,256]{2,1,0:T(4,128)(2,1)} %get-tuple-element.75), channel_id=1, source_target_pairs={{0,31},{1,24},{2,25},{3,26},{4,27},{5,28},{6,29},{7,30},{8,7},{9,0... | collective-permute-start | bytes 24584 | tf_op jit(solution)/shard_map/ppermute | solution.py:1060
  138.7 13.0 %collective-permute-start.9 = (bf16[4,48,256]{2,1,0:T(8,128)(2,1)}, bf16[4,48,256]{2,1,0:T(8,128)(2,1)S(1)}, u32[]{:S(2)}, u32[]{:S(2)}) collective-permute-start(bf16[4,48,256]{2,1,0:T(8,128)(2,1)} %get-tuple-element.78), channel_id=1, source_target_pairs={{0,8},{1,9},{2,10},{3,11},{4,12},{5,13},{6,14},{7,15},{8,16},{9,17... | collective-permute-start | bytes 294920 | tf_op jit(solution)/shard_map/ppermute | solution.py:1060
  141.7 10.1 %collective-permute-start.10 = (bf16[16,4,256]{2,1,0:T(4,128)(2,1)}, bf16[16,4,256]{2,1,0:T(4,128)(2,1)S(1)}, u32[]{:S(2)}, u32[]{:S(2)}) collective-permute-start(bf16[16,4,256]{2,1,0:T(4,128)(2,1)} %get-tuple-element.79), channel_id=1, source_target_pairs={{0,1},{1,2},{2,3},{3,4},{4,5},{5,6},{6,7},{7,0},{8,9},{9,10},{10,1... | collective-permute-start | bytes 98312 | tf_op jit(solution)/shard_map/ppermute | solution.py:1060
  144.9 6.9 %collective-permute-start.11 = (bf16[4,4,256]{2,1,0:T(4,128)(2,1)}, bf16[4,4,256]{2,1,0:T(4,128)(2,1)S(1)}, u32[]{:S(2)}, u32[]{:S(2)}) collective-permute-start(bf16[4,4,256]{2,1,0:T(4,128)(2,1)} %get-tuple-element.80), channel_id=1, source_target_pairs={{0,9},{1,10},{2,11},{3,12},{4,13},{5,14},{6,15},{7,8},{8,17},{9,18... | collective-permute-start | bytes 24584 | tf_op jit(solution)/shard_map/ppermute | solution.py:1060
where the time goes:
time: 167 us; the launch traced here: 166 us
  Pallas kernels  80.9 us (48%)
  blocking collectives  45.2 us (27%)
  starting transfers between devices  23.5 us (14%)
  waiting for transfers between devices  15.3 us (9%)
    pallas_call x7, Pallas kernels, staged(): pl.pallas_call(kernel, out_shape=tuple((pltpu.HBM(o.shape, o.dtype) for o...  80.9 us
    all_to_all x2, blocking collectives, exchange(): lax.all_to_all(x, ('lat', 'lon'), split_axis=0, concat_axis=0, tiled=True)  45.2 us
    ppermute x12, starting transfers between devices, neighbour(): return lax.ppermute(x, ('lat', 'lon'), pairs)  20.9 us
    ppermute x12, waiting for transfers between devices, neighbour(): return lax.ppermute(x, ('lat', 'lon'), pairs)  15.3 us
  transfers between devices with their start and end apart: 13, of which 4 were waited for; matrix products, arithmetic and copies ran while one was open for 0% of the time, Pallas kernels for 25%

commit v1 on v0

--- a/solution.py
+++ b/solution.py
@@ -323,13 +323,13 @@
 
 
 def split(cap):
-    first = max(8, cap // 4)
-    return (first, first, cap - 2 * first), min(16, first)
+    first = cap // 2
+    return (first, cap - first), min(16, first)
 
 
 def route_kernel(
     parts, stage, count_ref, owner_ref, point_ref, r_ref, w2_ref, values_ref,
-    send1_ref, send2_ref, send3_ref, mixed_ref, y_ref, buf_ref, tgt_ref, tgt_smem, sem,
+    send1_ref, send2_ref, mixed_ref, y_ref, buf_ref, tgt_ref, tgt_smem, sem,
 ):
     cap = sum(parts)
     slots = owner_ref.shape[1]
@@ -396,20 +396,22 @@
         return 0
 
     lax.fori_loop(0, chunks, move, 0)
+    fill = ((0, 0), (0, LANES - cap))
+    codes = jnp.concatenate([jnp.pad(high, fill), jnp.pad(low, fill)], axis=1)
+    stage.emit(mixed_ref)
     for d in range(devices):
         offset = d * cap
-        for ref, size in zip((send1_ref, send2_ref, send3_ref), parts):
+        for ref, size in zip((send1_ref, send2_ref), parts):
             for half in range(2):
                 ref[d, 0:size, half * LANES : (half + 1) * LANES] = buf_ref[
                     half, offset : offset + size, :
                 ].astype(BF)
             offset += size
-    fill = ((0, 0), (0, LANES - cap))
-    codes = jnp.concatenate([jnp.pad(high, fill), jnp.pad(low, fill)], axis=1)
-    for d in range(devices):
         send1_ref[d, parts[0] : parts[0] + EXTRA, :] = jnp.broadcast_to(
             codes[d : d + 1], (EXTRA, 2 * LANES)
         ).astype(BF)
+        if (d + 1) % 8 == 0:
+            stage.emit_part(pl.ds(d - 7, 8), send1_ref, send2_ref)
 
 
 def route(owner, point, count, values, r_inverse, w2, devices, parts):
@@ -700,9 +702,9 @@
 
 def forecast_kernel(
     parts, group, stage, obs1_ref, h1_ref, ans_ref, above_ref, west_ref, corner_ref, gain_ref,
-    wup_ref, wdown_ref, whead_ref, state_ref, w1_in_ref, mixed_ref, obs2_ref, back_ref, inv_ref,
-    h2_ref, gp_ref, prior_ref, found3_ref, idx_ref, cnt_ref, dup_ref, pulled_ref, w1_ref,
-    pad_ref, table_ref, moved_ref, found1_ref, found2_ref, idx_smem, cnt_smem, dup_smem, sems,
+    wup_ref, wdown_ref, whead_ref, state_ref, w1_in_ref, mixed_ref, back_ref, inv_ref,
+    h2_ref, gp_ref, prior_ref, found2_ref, idx_ref, cnt_ref, dup_ref, pulled_ref, w1_ref,
+    pad_ref, table_ref, moved_ref, found1_ref, idx_smem, cnt_smem, dup_smem, sems,
 ):
     rows, cols, width = h1_ref.shape
     devices = obs1_ref.shape[0]
@@ -763,22 +765,20 @@
 
     lax.fori_loop(0, 2, forward, 0)
     stage.emit(h2_ref, gp_ref, idx_ref, cnt_ref, dup_ref)
-    stage.need(back_ref, inv_ref, w1_in_ref, mixed_ref, obs2_ref)
+    stage.need(back_ref, inv_ref, w1_in_ref, mixed_ref)
     w1_ref[...] = jnp.zeros_like(w1_ref)
     w1_ref[0:VARS, :] = w1_in_ref[...]
     w1_ref[...] = w1_ref[...].astype(BF).astype(F32)
     for copy in copies:
         copy.wait()
-    offsets = (0, parts[0], parts[0] + parts[1])
-    founds = (found1_ref, found2_ref, found3_ref)
+    offsets = (0, parts[0])
+    founds = (found1_ref, found2_ref)
     for offset, size, found in zip(offsets, parts, founds):
         gather_part(table_ref, found, idx_smem, cnt_smem, offset, size, group)
-    stage.emit(found3_ref)
+    stage.emit(found2_ref)
     table_ref[...] = jnp.zeros_like(table_ref)
     radiance_part(found1_ref, obs1_ref, mixed_ref, w1_ref, parts[0])
     scatter_part(table_ref, found1_ref, idx_smem, cnt_smem, dup_smem, 0, parts[0], group)
-    radiance_part(found2_ref, obs2_ref, mixed_ref, w1_ref, parts[1])
-    scatter_part(table_ref, found2_ref, idx_smem, cnt_smem, dup_smem, parts[0], parts[1], group)
 
     def collect(i, _):
         here = pl.ds(pl.multiple_of(i * step, step), step)
@@ -794,8 +794,8 @@
 
 
 def forecast(
-    h1, ans, above, west, corner, state, background, inv, obs1, obs2, mixed, gains, wup, wdown,
-    whead, w1, parts, group,
+    h1, ans, above, west, corner, state, background, inv, obs1, mixed, gains, wup, wdown, whead,
+    w1, parts, group,
 ):
     rows, cols, width = h1.shape
     tokens = rows * cols
@@ -805,7 +805,7 @@
         sh((tokens, width), F32),
         sh((tokens, wup.shape[2]), BF),
         sh(state.shape, F32),
-        sh((devices * parts[2], LANES), F32),
+        sh((devices * parts[1], LANES), F32),
         sh((devices, LANES), jnp.int32),
         sh((devices, LANES), jnp.int32),
         sh((devices, LANES), jnp.int32),
@@ -815,7 +815,7 @@
     return staged(
         functools.partial(forecast_kernel, parts, group),
         (
-            obs1, h1, ans, above, west, corner, gains, wup, wdown, whead, state, w1, mixed, obs2,
+            obs1, h1, ans, above, west, corner, gains, wup, wdown, whead, state, w1, mixed,
             background, inv,
         ),
         outs,
@@ -824,18 +824,17 @@
             pltpu.VMEM((PIX * tokens + group, LANES), F32),
             pltpu.VMEM((tokens // 2, state.shape[1]), F32),
             pltpu.VMEM((devices * parts[0], LANES), F32),
-            pltpu.VMEM((devices * parts[1], LANES), F32),
         ]
         + [pltpu.SMEM((devices, LANES), jnp.int32)] * 3
         + [pltpu.SemaphoreType.DMA((3,))],
         3e9,
-        vmem=(0, 3, 4, 5, 13),
+        vmem=(0, 3, 4, 5),
         layer={7: 1, 8: 1},
     )
 
 
 def adjoint_kernel(
-    parts, group, stage, idx_smem, cnt_smem, dup_smem, w1_ref, mixed_ref, work_ref, obs3_ref,
+    parts, group, stage, idx_smem, cnt_smem, dup_smem, w1_ref, mixed_ref, work_ref, obs2_ref,
     whead_ref, pulled_ref, prior_ref, wdown_ref, gp_ref, wup_ref, h2_ref, gain_ref,
     top_ref, left_ref, edge_ref, third_ref, out_ref, table_ref, moved_ref,
 ):
@@ -843,10 +842,10 @@
     tokens = rows * cols
     step = tokens // 2
     table_ref[...] = jnp.zeros_like(table_ref)
-    stage.need(idx_smem, cnt_smem, dup_smem, w1_ref, mixed_ref, work_ref, obs3_ref)
-    radiance_part(work_ref, obs3_ref, mixed_ref, w1_ref, parts[2])
+    stage.need(idx_smem, cnt_smem, dup_smem, w1_ref, mixed_ref, work_ref, obs2_ref)
+    radiance_part(work_ref, obs2_ref, mixed_ref, w1_ref, parts[1])
     scatter_part(
-        table_ref, work_ref, idx_smem, cnt_smem, dup_smem, parts[0] + parts[1], parts[2], group
+        table_ref, work_ref, idx_smem, cnt_smem, dup_smem, parts[0], parts[1], group
     )
     stage.need(whead_ref, pulled_ref, prior_ref, wdown_ref, gp_ref, wup_ref, h2_ref, gain_ref)
     half = rows // 2
@@ -872,7 +871,7 @@
 
 
 def adjoint(
-    idx, cnt, dup, found, obs3, mixed, w1, h2, gp, gains, wup, wdown, whead, prior, pulled, parts,
+    idx, cnt, dup, found, obs2, mixed, w1, h2, gp, gains, wup, wdown, whead, prior, pulled, parts,
     group, rows, cols,
 ):
     width = h2.shape[1]
@@ -880,7 +879,7 @@
     outs = (top, left, edge, third, jax.ShapeDtypeStruct(prior.shape, F32))
     return staged(
         functools.partial(adjoint_kernel, parts, group),
-        (idx, cnt, dup, w1, mixed, found, obs3, whead, pulled, prior, wdown, gp, wup, h2, gains),
+        (idx, cnt, dup, w1, mixed, found, obs2, whead, pulled, prior, wdown, gp, wup, h2, gains),
         outs,
         [
             pltpu.VMEM((PIX * rows * cols + group, LANES), F32),
@@ -1094,7 +1093,7 @@
 
     parts, group = split(cap)
 
-    send1, send2, send3, mixed = route(
+    send1, send2, mixed = route(
         obs_owner.reshape(1, slots), obs_point.reshape(1, slots), obs_count, obs_values,
         r_inverse, w_obs2, devices, parts,
     )
@@ -1108,24 +1107,22 @@
     below = neighbour(top.reshape(SHIFT, cols, width), -1, 0)
     right = neighbour(left.reshape(rows, SHIFT, width), 0, -1)
     corner = neighbour(corner, -1, -1)
-    obs1, send2 = lax.optimization_barrier((obs1, send2))
-    obs2 = exchange(send2)
     answer, low, east, last, qkv1 = shifted_forward(
         row_start, z1, right, below, corner, w_qkv, w_proj, head_scale, total_rows
     )
     above = neighbour(low, 1, 0)
     west = neighbour(east, 0, 1)
     last = neighbour(last, 1, 1)
-    obs2, send3 = lax.optimization_barrier((obs2, send3))
-    obs3 = exchange(send3)
+    obs1, send2 = lax.optimization_barrier((obs1, send2))
+    obs2 = exchange(send2)
     flat = (rows * cols, patch_values)
     h2, gp1, prior, found, idx, cnt, dup, pulled, w1 = forecast(
         h1, answer, above, west, last, state.reshape(flat), background.reshape(flat),
-        inv_background, obs1, obs2, mixed, norm_gain, w_up, w_down, w_head.T,
+        inv_background, obs1, mixed, norm_gain, w_up, w_down, w_head.T,
         w_obs1, parts, group,
     )
     top, left, corner, third, partial = adjoint(
-        idx, cnt, dup, found, obs3, mixed, w1, h2, gp1, norm_gain, w_up, w_down, w_head.T, prior,
+        idx, cnt, dup, found, obs2, mixed, w1, h2, gp1, norm_gain, w_up, w_down, w_head.T, prior,
         pulled,
         parts, group, rows, cols,
     )

time: 167 us -> 158 us (0.946)
  blocking collectives: 45.2 us -> 37.7 us
    all_to_all x2 -> x1, blocking collectives: 45.2 us -> 37.7 us  [exchange(): lax.all_to_all(x, ('lat', 'lon'), split_axis=0, concat_axis=0, tiled=True)]
  transfers between devices with their start and end apart: 13 -> 13, of which waited for: 4 -> 4; matrix products, arithmetic and copies ran while one was open for 0% -> 0% of each run, Pallas kernels for 25% -> 26%
where the time goes in v1:
time: 158 us
  Pallas kernels  80.1 us (51%)
  blocking collectives  37.7 us (24%)
  starting transfers between devices  23.5 us (15%)
  waiting for transfers between devices  15.4 us (10%)
    pallas_call x7, Pallas kernels, staged(): pl.pallas_call(kernel, out_shape=tuple((pltpu.HBM(o.shape, o.dtype) for o...  80.1 us
    all_to_all x1, blocking collectives, exchange(): lax.all_to_all(x, ('lat', 'lon'), split_axis=0, concat_axis=0, tiled=True)  37.7 us
    ppermute x12, starting transfers between devices, neighbour(): return lax.ppermute(x, ('lat', 'lon'), pairs)  20.9 us
    ppermute x12, waiting for transfers between devices, neighbour(): return lax.ppermute(x, ('lat', 'lon'), pairs)  15.4 us
  transfers between devices with their start and end apart: 13, of which 4 were waited for; matrix products, arithmetic and copies ran while one was open for 0% of the time, Pallas kernels for 26%

profile of v1, /device:TPU:0, one launch (start us, length us, event | category | flops | bytes accessed | tf_op | source)
XLA Modules:
  0.0 157.9 jit_solution(12101952094495894873)
XLA Ops:
  0.7 7.2 %shard_map.172 = (bf16[32,72,256]{2,1,0:T(8,128)(2,1)}, bf16[32,64,256]{2,1,0:T(8,128)(2,1)}, bf16[256,256]{1,0:T(8,128)(2,1)}) custom-call(s32[1]{0:T(128)S(6)} %copy.19.refs_0_, s32[1,2048]{1,0:T(1,128)} %bitcast.22, s32[1,2048]{1,0:T(1,128)} %bitcast.23, f32[256,256]{1,0:T(8,128)} %refs_3_.2, f32[256,256]{1,0:T(8,128)} %refs_4_.2, f32[2048,256]{1,0:T(8,128)} %refs_5_.2), custom_call_target="tpu_custom_call" | custom-call | flops 1000000000 | bytes 8388608 | tf_op jit(solution)/shard_map/pallas_call | solution.py:137
  7.9 0.0 copy-start.11
  7.9 37.7 %all_to_all.10.refs_0_ = bf16[32,72,256]{2,1,0:T(8,128)(2,1)S(1)} all-to-all(bf16[32,72,256]{2,1,0:T(8,128)(2,1)} %get-tuple-element.42), channel_id=1, replica_groups=mesh['lat'=4,'lon'=8] {'lat','lon'}, dimensions={0} | all-to-all | bytes 2359296 | tf_op jit(solution)/shard_map/all_to_all | solution.py:1063
  45.6 2.6 %all-to-all-start.1 = ((bf16[32,64,256]{2,1,0:T(8,128)(2,1)}), bf16[32,64,256]{2,1,0:T(8,128)(2,1)S(1)}, u32[]{:S(2)}, u32[]{:S(2)}) async-start(bf16[32,64,256]{2,1,0:T(8,128)(2,1)} %get-tuple-element.60), calls=%async_computation.1 | async-start | bytes 2097152 | tf_op jit(solution)/shard_map/all_to_all | solution.py:1063
  48.2 0.0 copy-done.11
  48.3 12.3 %shard_map.173 = (bf16[4,6,8,256]{3,2,1,0:T(8,128)(2,1)}, bf16[2,8,4,256]{3,2,1,0:T(4,128)(2,1)}, bf16[4,4,256]{2,1,0:T(4,128)(2,1)}, f32[2,8,6,8,256]{4,3,2,1,0...) custom-call(f32[2,8]{1,0:T(2,128)S(1)} %copy-done.11, ...), custom_call_target="tpu_custom_call" | custom-call | flops 2000000000 | bytes 8388608 | tf_op jit(solution)/shard_map/pallas_call | solution.py:137
  60.6 2.6 %collective-permute-start.1 = (bf16[4,48,256]{2,1,0:T(8,128)(2,1)}, bf16[4,48,256]{2,1,0:T(8,128)(2,1)S(1)}, u32[]{:S(2)}, u32[]{:S(2)}) collective-permute-start(bf16[4,48,256]{2,1,0:T(8,128)(2,1)} %bitcast.20), channel_id=1, source_target_pairs={{0,24},{1,25},{2,26},{3,27},{4,28},{5,29},{6,30},{7,31},{8,0},{9,1... | collective-permute-start | bytes 294920 | tf_op jit(solution)/shard_map/ppermute | solution.py:1059
  63.2 2.9 %collective-permute-start = (bf16[16,4,256]{2,1,0:T(4,128)(2,1)}, bf16[16,4,256]{2,1,0:T(4,128)(2,1)S(1)}, u32[]{:S(2)}, u32[]{:S(2)}) collective-permute-start(bf16[16,4,256]{2,1,0:T(4,128)(2,1)} %bitcast.21), channel_id=1, source_target_pairs={{0,7},{1,0},{2,1},{3,2},{4,3},{5,4},{6,5},{7,6},{8,15},{9,8},{10,9... | collective-permute-start | bytes 98312 | tf_op jit(solution)/shard_map/ppermute | solution.py:1059
  66.1 0.6 collective-permute-start.2
  66.8 2.7 %collective-permute-done.2.refs_5_ = bf16[4,4,256]{2,1,0:T(4,128)(2,1)S(1)} collective-permute-done((bf16[4,4,256]{2,1,0:T(4,128)(2,1)}, bf16[4,4,256]{2,1,0:T(4,128)(2,1)S(1)}, u32[]{:S(2)}, u32[]{:S(2)}) %collective-permute-start.2) | collective-permute-done | bytes 8224 | tf_op jit(solution)/shard_map/ppermute | solution.py:1059
  69.5 0.0 collective-permute-done.refs_3_
  69.5 0.0 collective-permute-done.1.refs_4_
  69.5 6.3 %shard_map.174 = (f32[16,48,256]{2,1,0:T(8,128)}, bf16[4,48,256]{2,1,0:T(8,128)(2,1)}, bf16[16,4,256]{2,1,0:T(4,128)(2,1)}, bf16[4,4,256]{2,1,0:T(4,128)(2,1)}, bf16[768,768]{1,0:T(8,128)(2,1)}) custom-call(s32[1]{0:T(128)} %bitcast.4.refs_0_, f32[2,8]{1,0:T(2,128)S(1)} %copy-done.11, f32[16,48,256]{2,1,0:T(8,128)} %bitcast.24, ...), custom_call_target="tpu_custom_call" | custom-call | flops 1000000000 | bytes 8388608 | tf_op jit(solution)/shard_map/pallas_call | solution.py:137
  75.7 1.0 collective-permute-start.3
  76.7 0.0 collective-permute-start.4
  76.7 1.1 collective-permute-start.5
  77.8 5.8 %collective-permute-done.5.refs_5_ = bf16[4,4,256]{2,1,0:T(4,128)(2,1)S(1)} collective-permute-done((bf16[4,4,256]{2,1,0:T(4,128)(2,1)}, bf16[4,4,256]{2,1,0:T(4,128)(2,1)S(1)}, u32[]{:S(2)}, u32[]{:S(2)}) %collective-permute-start.5) | collective-permute-done | bytes 8224 | tf_op jit(solution)/shard_map/ppermute | solution.py:1059
  83.6 0.0 collective-permute-done.4.refs_4_
  83.6 0.0 collective-permute-done.3.refs_3_
  83.6 21.9 %shard_map.175 = (f32[768,256]{1,0:T(8,128)}, bf16[768,1024]{1,0:T(8,128)(2,1)}, f32[768,1104]{1,0:T(8,128)}, f32[2048,128]{1,0:T(8,128)}, s32[32,128]{1,0:T(8,1...) custom-call(bf16[32,72,256]{2,1,0:T(8,128)(2,1)S(1)} %all_to_all.10.refs_0_, ...), custom_call_target="tpu_custom_call" | custom-call | flops 3000000000 | bytes 8388608 | tf_op jit(solution)/shard_map/pallas_call | solution.py:137
  105.4 0.0 all-to-all-done.1.refs_6_
  105.5 0.0 copy-start.5
  105.5 0.0 copy-start.9
  105.5 0.0 copy-start.12
  105.5 0.0 copy-start.3
  105.5 0.0 copy-start.4
  105.5 0.0 copy-start.7
  105.5 0.0 copy-start.8
  105.5 10.1 %shard_map.176 = (bf16[4,48,256]{2,1,0:T(8,128)(2,1)}, bf16[16,4,256]{2,1,0:T(4,128)(2,1)}, bf16[4,4,256]{2,1,0:T(4,128)(2,1)}, f32[16,48,256]{2,1,0:T(8,128)}, f32[768,1104]{1,0:T(8,128)}) custom-call(s32[32,128]{1,0:T(8,128)} %get-tuple-element.55.refs_0_, s32[32,128]{1,0:T(8,128)} %get-tuple-element.56.refs_1_, s32[32,128]{1,0:T(8,128)} %get-tuple-element.57.refs_2_, ...), custom_call_target="tpu_custom_call" | custom-call | flops 2000000000 | bytes 8388608 | tf_op jit(solution)/shard_map/pallas_call | solution.py:137
  115.7 0.0 copy-start
  115.7 0.0 copy-start.1
  115.7 0.0 copy-start.2
  115.7 0.0 copy-start.10
  115.7 0.1 collective-permute-start.7
  115.8 3.2 %collective-permute-start.6 = (bf16[16,4,256]{2,1,0:T(4,128)(2,1)}, bf16[16,4,256]{2,1,0:T(4,128)(2,1)S(1)}, u32[]{:S(2)}, u32[]{:S(2)}) collective-permute-start(bf16[16,4,256]{2,1,0:T(4,128)(2,1)} %get-tuple-element.67), channel_id=1, source_target_pairs={{0,7},{1,0},{2,1},{3,2},{4,3},{5,4},{6,5},{7,6},{8,15},{9,8},{10,9... | collective-permute-start | bytes 98312 | tf_op jit(solution)/shard_map/ppermute | solution.py:1059
  118.9 0.0 collective-permute-start.8
  118.9 3.3 %collective-permute-done.8.refs_5_ = bf16[4,4,256]{2,1,0:T(4,128)(2,1)S(1)} collective-permute-done((bf16[4,4,256]{2,1,0:T(4,128)(2,1)}, bf16[4,4,256]{2,1,0:T(4,128)(2,1)S(1)}, u32[]{:S(2)}, u32[]{:S(2)}) %collective-permute-start.8) | collective-permute-done | bytes 8224 | tf_op jit(solution)/shard_map/ppermute | solution.py:1059
  122.2 0.0 collective-permute-done.6.refs_3_
  122.2 0.0 collective-permute-done.7.refs_4_
  122.2 0.0 copy-done.5
  122.2 8.3 %shard_map.177 = (f32[16,48,256]{2,1,0:T(8,128)}, bf16[4,48,256]{2,1,0:T(8,128)(2,1)}, bf16[16,4,256]{2,1,0:T(4,128)(2,1)}, bf16[4,4,256]{2,1,0:T(4,128)(2,1)}) custom-call(s32[1]{0:T(128)} %bitcast.4.refs_0_, f32[2,8]{1,0:T(2,128)S(1)} %copy-done.11, f32[16,48,256]{2,1,0:T(8,128)} %get-tuple-element.66.refs_2_.refs_6_, ...), custom_call_target="tpu_custom_call" | custom-call | flops 1000000000 | bytes 8388608 | tf_op jit(solution)/shard_map/pallas_call | solution.py:137
  130.5 2.9 %collective-permute-start.9 = (bf16[4,48,256]{2,1,0:T(8,128)(2,1)}, bf16[4,48,256]{2,1,0:T(8,128)(2,1)S(1)}, u32[]{:S(2)}, u32[]{:S(2)}) collective-permute-start(bf16[4,48,256]{2,1,0:T(8,128)(2,1)} %get-tuple-element.72), channel_id=1, source_target_pairs={{0,8},{1,9},{2,10},{3,11},{4,12},{5,13},{6,14},{7,15},{8,16},{9,17... | collective-permute-start | bytes 294920 | tf_op jit(solution)/shard_map/ppermute | solution.py:1059
  133.4 3.2 %collective-permute-start.10 = (bf16[16,4,256]{2,1,0:T(4,128)(2,1)}, bf16[16,4,256]{2,1,0:T(4,128)(2,1)S(1)}, u32[]{:S(2)}, u32[]{:S(2)}) collective-permute-start(bf16[16,4,256]{2,1,0:T(4,128)(2,1)} %get-tuple-element.73), channel_id=1, source_target_pairs={{0,1},{1,2},{2,3},{3,4},{4,5},{5,6},{6,7},{7,0},{8,9},{9,10},{10,1... | collective-permute-start | bytes 98312 | tf_op jit(solution)/shard_map/ppermute | solution.py:1059
  136.6 3.3 %collective-permute-start.11 = (bf16[4,4,256]{2,1,0:T(4,128)(2,1)}, bf16[4,4,256]{2,1,0:T(4,128)(2,1)S(1)}, u32[]{:S(2)}, u32[]{:S(2)}) collective-permute-start(bf16[4,4,256]{2,1,0:T(4,128)(2,1)} %get-tuple-element.74), channel_id=1, source_target_pairs={{0,9},{1,10},{2,11},{3,12},{4,13},{5,14},{6,15},{7,8},{8,17},{9,18... | collective-permute-start | bytes 24584 | tf_op jit(solution)/shard_map/ppermute | solution.py:1059
  139.9 3.6 %collective-permute-done.11.refs_5_ = bf16[4,4,256]{2,1,0:T(4,128)(2,1)S(1)} collective-permute-done((bf16[4,4,256]{2,1,0:T(4,128)(2,1)}, bf16[4,4,256]{2,1,0:T(4,128)(2,1)S(1)}, u32[]{:S(2)}, u32[]{:S(2)}) %collective-permute-start.11) | collective-permute-done | bytes 8224 | tf_op jit(solution)/shard_map/ppermute | solution.py:1059
  143.5 0.0 collective-permute-done.10.refs_4_
  143.5 0.0 collective-permute-done.9.refs_3_
  143.6 14.1 %shard_map.178 = f32[16,48,1104]{2,1,0:T(8,128)} custom-call(f32[2,8]{1,0:T(2,128)S(1)} %copy-done.11, f32[16,48,1104]{2,1,0:T(8,128)} %bitcast.17, f32[16,48,256]{2,1,0:T(8,128)} %get-tuple-element.71.refs_2_, bf16[4,48,256]{2,1,0:T(8,128)(2,1)S(1)} %collective-permute-done.9.refs_3_, bf16[16,4,256]{2,1,0:T(4,128)(2,1)S(1)} %collective-permute-done.10.refs_4_, ...), custom_call_target="tpu_custom_call" | custom-call | flops 2000000000 | bytes 8388608 | tf_op jit(solution)/shard_map/pallas_call | solution.py:137
  (12 shorter events, 0.0 us)
Async XLA Ops:
  7.9 40.4 %copy-start.11 = (f32[2,8]{1,0:T(2,128)S(1)}, f32[2,8]{1,0:T(2,128)}, u32[]{:S(2)}) copy-start(f32[2,8]{1,0:T(2,128)} %refs_0_.4) | copy-start | bytes 196
  45.6 59.9 %all-to-all-start.1 = ((bf16[32,64,256]{2,1,0:T(8,128)(2,1)}), bf16[32,64,256]{2,1,0:T(8,128)(2,1)S(1)}, u32[]{:S(2)}, u32[]{:S(2)}) async-start(bf16[32,64,256]{2,1,0:T(8,128)(2,1)} %get-tuple-element.60), calls=%async_computation.1 | async-start | bytes 2097152 | tf_op jit(solution)/shard_map/all_to_all | solution.py:1063
  60.6 8.9 %collective-permute-start.1 = (bf16[4,48,256]{2,1,0:T(8,128)(2,1)}, bf16[4,48,256]{2,1,0:T(8,128)(2,1)S(1)}, u32[]{:S(2)}, u32[]{:S(2)}) collective-permute-start(bf16[4,48,256]{2,1,0:T(8,128)(2,1)} %bitcast.20), channel_id=1, source_target_pairs={{0,24},{1,25},{2,26},{3,27},{4,28},{5,29},{6,30},{7,31},{8,0},{9,1... | collective-permute-start | bytes 294920 | tf_op jit(solution)/shard_map/ppermute | solution.py:1059
  63.2 6.3 %collective-permute-start = (bf16[16,4,256]{2,1,0:T(4,128)(2,1)}, bf16[16,4,256]{2,1,0:T(4,128)(2,1)S(1)}, u32[]{:S(2)}, u32[]{:S(2)}) collective-permute-start(bf16[16,4,256]{2,1,0:T(4,128)(2,1)} %bitcast.21), channel_id=1, source_target_pairs={{0,7},{1,0},{2,1},{3,2},{4,3},{5,4},{6,5},{7,6},{8,15},{9,8},{10,9... | collective-permute-start | bytes 98312 | tf_op jit(solution)/shard_map/ppermute | solution.py:1059
  66.1 3.3 %collective-permute-start.2 = (bf16[4,4,256]{2,1,0:T(4,128)(2,1)}, bf16[4,4,256]{2,1,0:T(4,128)(2,1)S(1)}, u32[]{:S(2)}, u32[]{:S(2)}) collective-permute-start(bf16[4,4,256]{2,1,0:T(4,128)(2,1)} %get-tuple-element.50), channel_id=1, source_target_pairs={{0,31},{1,24},{2,25},{3,26},{4,27},{5,28},{6,29},{7,30},{8,7},{9,0... | collective-permute-start | bytes 24584 | tf_op jit(solution)/shard_map/ppermute | solution.py:1059
  75.7 7.9 %collective-permute-start.3 = (bf16[4,48,256]{2,1,0:T(8,128)(2,1)}, bf16[4,48,256]{2,1,0:T(8,128)(2,1)S(1)}, u32[]{:S(2)}, u32[]{:S(2)}) collective-permute-start(bf16[4,48,256]{2,1,0:T(8,128)(2,1)} %get-tuple-element.52), channel_id=1, source_target_pairs={{0,8},{1,9},{2,10},{3,11},{4,12},{5,13},{6,14},{7,15},{8,16},{9,17... | collective-permute-start | bytes 294920 | tf_op jit(solution)/shard_map/ppermute | solution.py:1059
  76.7 6.9 %collective-permute-start.4 = (bf16[16,4,256]{2,1,0:T(4,128)(2,1)}, bf16[16,4,256]{2,1,0:T(4,128)(2,1)S(1)}, u32[]{:S(2)}, u32[]{:S(2)}) collective-permute-start(bf16[16,4,256]{2,1,0:T(4,128)(2,1)} %get-tuple-element.53), channel_id=1, source_target_pairs={{0,1},{1,2},{2,3},{3,4},{4,5},{5,6},{6,7},{7,0},{8,9},{9,10},{10,1... | collective-permute-start | bytes 98312 | tf_op jit(solution)/shard_map/ppermute | solution.py:1059
  76.7 6.9 %collective-permute-start.5 = (bf16[4,4,256]{2,1,0:T(4,128)(2,1)}, bf16[4,4,256]{2,1,0:T(4,128)(2,1)S(1)}, u32[]{:S(2)}, u32[]{:S(2)}) collective-permute-start(bf16[4,4,256]{2,1,0:T(4,128)(2,1)} %get-tuple-element.54), channel_id=1, source_target_pairs={{0,9},{1,10},{2,11},{3,12},{4,13},{5,14},{6,15},{7,8},{8,17},{9,18... | collective-permute-start | bytes 24584 | tf_op jit(solution)/shard_map/ppermute | solution.py:1059
  105.5 16.8 %copy-start.5 = (bf16[2,256,768]{2,1,0:T(8,128)(2,1)S(1)}, bf16[2,256,768]{2,1,0:T(8,128)(2,1)}, u32[]{:S(2)}) copy-start(bf16[2,256,768]{2,1,0:T(8,128)(2,1)} %refs_15_.1) | copy-start | bytes 2359300
  105.5 16.8 %copy-start.9 = (bf16[2,256,256]{2,1,0:T(8,128)(2,1)S(1)}, bf16[2,256,256]{2,1,0:T(8,128)(2,1)}, u32[]{:S(2)}) copy-start(bf16[2,256,256]{2,1,0:T(8,128)(2,1)} %refs_13_.1) | copy-start | bytes 786436
  105.5 16.8 %copy-start.12 = (bf16[768,768]{1,0:T(8,128)(2,1)S(1)}, bf16[768,768]{1,0:T(8,128)(2,1)}, u32[]{:S(2)}) copy-start(bf16[768,768]{1,0:T(8,128)(2,1)} %get-tuple-element.70.refs_7_) | copy-start | bytes 3538948
  105.5 38.0 %copy-start.3 = (bf16[768,1024]{1,0:T(8,128)(2,1)S(1)}, bf16[768,1024]{1,0:T(8,128)(2,1)}, u32[]{:S(2)}) copy-start(bf16[768,1024]{1,0:T(8,128)(2,1)} %get-tuple-element.75.refs_10_) | copy-start | bytes 4718596
  105.5 38.0 %copy-start.4 = (bf16[768,768]{1,0:T(8,128)(2,1)S(1)}, bf16[768,768]{1,0:T(8,128)(2,1)}, u32[]{:S(2)}) copy-start(bf16[768,768]{1,0:T(8,128)(2,1)} %get-tuple-element.77.refs_14_) | copy-start | bytes 3538948
  105.5 38.0 %copy-start.7 = (f32[768,256]{1,0:T(8,128)S(1)}, f32[768,256]{1,0:T(8,128)}, u32[]{:S(2)}) copy-start(f32[768,256]{1,0:T(8,128)} %get-tuple-element.76.refs_12_) | copy-start | bytes 2359300
  105.5 38.0 %copy-start.8 = (bf16[1104,256]{1,0:T(8,128)(2,1)S(1)}, bf16[1104,256]{1,0:T(8,128)(2,1)}, u32[]{:S(2)}) copy-start(bf16[1104,256]{1,0:T(8,128)(2,1)} %refs_17_.1) | copy-start | bytes 1695748
  115.7 27.9 %copy-start = (bf16[2,256,1024]{2,1,0:T(8,128)(2,1)S(1)}, bf16[2,256,1024]{2,1,0:T(8,128)(2,1)}, u32[]{:S(2)}) copy-start(bf16[2,256,1024]{2,1,0:T(8,128)(2,1)} %refs_11_.3) | copy-start | bytes 3145732
  115.7 27.9 %copy-start.1 = (bf16[2,1024,256]{2,1,0:T(8,128)(2,1)S(1)}, bf16[2,1024,256]{2,1,0:T(8,128)(2,1)}, u32[]{:S(2)}) copy-start(bf16[2,1024,256]{2,1,0:T(8,128)(2,1)} %refs_9_.1) | copy-start | bytes 3145732
  115.7 27.9 %copy-start.2 = (f32[2,8,6,8,256]{4,3,2,1,0:T(8,128)S(1)}, f32[2,8,6,8,256]{4,3,2,1,0:T(8,128)}, u32[]{:S(2)}) copy-start(f32[2,8,6,8,256]{4,3,2,1,0:T(8,128)} %get-tuple-element.46) | copy-start | bytes 2359300
  115.7 27.9 %copy-start.6 = (f32[768,256]{1,0:T(8,128)S(1)}, f32[768,256]{1,0:T(8,128)}, u32[]{:S(2)}) copy-start(f32[768,256]{1,0:T(8,128)} %get-tuple-element.78.refs_16_) | copy-start | bytes 2359300
  115.7 27.9 %copy-start.10 = (f32[2,2,256]{2,1,0:T(2,128)S(1)}, f32[2,2,256]{2,1,0:T(2,128)}, u32[]{:S(2)}) copy-start(f32[2,2,256]{2,1,0:T(2,128)} %refs_8_.7) | copy-start | bytes 12292
  115.7 6.5 %collective-permute-start.7 = (bf16[4,48,256]{2,1,0:T(8,128)(2,1)}, bf16[4,48,256]{2,1,0:T(8,128)(2,1)S(1)}, u32[]{:S(2)}, u32[]{:S(2)}) collective-permute-start(bf16[4,48,256]{2,1,0:T(8,128)(2,1)} %get-tuple-element.68), channel_id=1, source_target_pairs={{0,24},{1,25},{2,26},{3,27},{4,28},{5,29},{6,30},{7,31},{8,0},{9,1... | collective-permute-start | bytes 294920 | tf_op jit(solution)/shard_map/ppermute | solution.py:1059
  115.8 6.4 %collective-permute-start.6 = (bf16[16,4,256]{2,1,0:T(4,128)(2,1)}, bf16[16,4,256]{2,1,0:T(4,128)(2,1)S(1)}, u32[]{:S(2)}, u32[]{:S(2)}) collective-permute-start(bf16[16,4,256]{2,1,0:T(4,128)(2,1)} %get-tuple-element.67), channel_id=1, source_target_pairs={{0,7},{1,0},{2,1},{3,2},{4,3},{5,4},{6,5},{7,6},{8,15},{9,8},{10,9... | collective-permute-start | bytes 98312 | tf_op jit(solution)/shard_map/ppermute | solution.py:1059
  118.9 3.3 %collective-permute-start.8 = (bf16[4,4,256]{2,1,0:T(4,128)(2,1)}, bf16[4,4,256]{2,1,0:T(4,128)(2,1)S(1)}, u32[]{:S(2)}, u32[]{:S(2)}) collective-permute-start(bf16[4,4,256]{2,1,0:T(4,128)(2,1)} %get-tuple-element.69), channel_id=1, source_target_pairs={{0,31},{1,24},{2,25},{3,26},{4,27},{5,28},{6,29},{7,30},{8,7},{9,0... | collective-permute-start | bytes 24584 | tf_op jit(solution)/shard_map/ppermute | solution.py:1059
  130.5 13.0 %collective-permute-start.9 = (bf16[4,48,256]{2,1,0:T(8,128)(2,1)}, bf16[4,48,256]{2,1,0:T(8,128)(2,1)S(1)}, u32[]{:S(2)}, u32[]{:S(2)}) collective-permute-start(bf16[4,48,256]{2,1,0:T(8,128)(2,1)} %get-tuple-element.72), channel_id=1, source_target_pairs={{0,8},{1,9},{2,10},{3,11},{4,12},{5,13},{6,14},{7,15},{8,16},{9,17... | collective-permute-start | bytes 294920 | tf_op jit(solution)/shard_map/ppermute | solution.py:1059
  133.4 10.1 %collective-permute-start.10 = (bf16[16,4,256]{2,1,0:T(4,128)(2,1)}, bf16[16,4,256]{2,1,0:T(4,128)(2,1)S(1)}, u32[]{:S(2)}, u32[]{:S(2)}) collective-permute-start(bf16[16,4,256]{2,1,0:T(4,128)(2,1)} %get-tuple-element.73), channel_id=1, source_target_pairs={{0,1},{1,2},{2,3},{3,4},{4,5},{5,6},{6,7},{7,0},{8,9},{9,10},{10,1... | collective-permute-start | bytes 98312 | tf_op jit(solution)/shard_map/ppermute | solution.py:1059
  136.6 6.9 %collective-permute-start.11 = (bf16[4,4,256]{2,1,0:T(4,128)(2,1)}, bf16[4,4,256]{2,1,0:T(4,128)(2,1)S(1)}, u32[]{:S(2)}, u32[]{:S(2)}) collective-permute-start(bf16[4,4,256]{2,1,0:T(4,128)(2,1)} %get-tuple-element.74), channel_id=1, source_target_pairs={{0,9},{1,10},{2,11},{3,12},{4,13},{5,14},{6,15},{7,8},{8,17},{9,18... | collective-permute-start | bytes 24584 | tf_op jit(solution)/shard_map/ppermute | solution.py:1059
